TPU v7x, 256 devices: a whole 4x4x8 slice. The times are simulated.
256 devices in a mesh: group: 8 (over z_hi, y), shard: 32 (over x, z_lo, core).
Axes of the slice: x: 4, y: 4, z: 8 (z_hi: 2, z_lo: 4; z = z_hi * 4 + z_lo), core: 2. Of those that a mesh axis runs over, the one named last changes fastest.
Arguments:
- gradients: bfloat16 [8, 32, 256, 8192], P('group', 'shard'), may hold values from -1.59375 to 1.59375
- momentum: float32 [8, 256, 8192], P('group', None, 'shard'), may hold values from -6 to 6
- master: float32 [256, 8192], P(None, 'shard'), may hold values from -0.6 to 0.6
- indices: int32 [8, 4, 128, 32], P('group', None, 'shard'), may hold values from 0 to 4095, as said below
Outputs:
- momentum_out: float32 [8, 256, 8192], P('group', None, 'shard')
- master_out: float32 [256, 8192], P(None, 'shard')
- params_full: bfloat16 [256, 8192], replicated
Inputs may be any that keep to these rules, and one draw needn't show every extreme that they name: `indices`: the 32 positions of one group and block are distinct.
All inputs are finite; a program needn't handle non-finite values.
Results may differ from a plain program's by a relative error of at most 0.001.
Values may be sent and summed in bfloat16 or wider, within the bound.
No kernel may reach another device: no remote copies, remote signals or barrier semaphores. Data moves between devices by JAX's collectives and lax.ppermute only.
A program may use at most 128 MiB of HBM per device.

v0:
```python
import jax
import jax.numpy as jnp
import numpy as np
from jax import lax
from jax.experimental import pallas as pl
from jax.experimental.pallas import tpu as pltpu
from jax.sharding import Mesh
from jax.sharding import PartitionSpec as P


BLOCK = 64
W = 256
SHARD = ("x", "z", "c")
DECAY = 0.9
STEP = 0.5
TOP = 32767.0
EXTRA = 8
PAIR_BOUND = 3.2
OCTET_BOUND = 12.8
HI = lax.Precision.HIGHEST


def cosine_blocks():
    k = np.arange(BLOCK, dtype=np.float64)[:, None]
    n = np.arange(BLOCK, dtype=np.float64)[None, :]
    table = np.cos(np.pi * (2 * n + 1) * k / (2 * BLOCK)) * np.where(k == 0, np.sqrt(1 / BLOCK), np.sqrt(2 / BLOCK))
    return np.kron(np.eye(W // BLOCK), table).astype(np.float32)


def swapped(value, axis, mask):
    size = lax.axis_size(axis)
    return lax.ppermute(value, axis, [(i, i ^ mask) for i in range(size)])


def encode(field, bound):
    top = jnp.max(jnp.abs(field), axis=0, keepdims=True)
    scale = jnp.clip(jnp.ceil(top * (TOP / bound)), 1.0, TOP)
    code = jnp.round(field * ((TOP * TOP / bound) / scale))
    return code.astype(jnp.int32).astype(jnp.int16), jnp.broadcast_to(scale, (EXTRA, field.shape[1])).astype(jnp.int32).astype(jnp.int16)


def decode(code, scale, bound):
    return code.astype(jnp.int32).astype(jnp.float32) * (scale.astype(jnp.int32).astype(jnp.float32) * (bound / (TOP * TOP)))


ANY = pl.BlockSpec(memory_space=pl.ANY)
VM = pl.BlockSpec(memory_space=pltpu.VMEM)
HB = pl.BlockSpec(memory_space=pltpu.HBM)
MIB = 1 << 20


def params(mib):
    return pltpu.CompilerParams(vmem_limit_bytes=mib * MIB)


def own_place():
    return [lax.axis_index(name) for name in ("x", "z", "c")]


def column(d, e, flip, place):
    return pl.multiple_of((((place[0] ^ d) * 4 + (place[1] ^ e)) * 2 + (place[2] ^ flip)) * W, W)


def pick_out(grad, wanted, after=()):
    def body(g, *refs):
        outs, sem = refs[len(after) : -1], refs[-1]
        place = own_place()
        copies = []
        for out, (zs, flip) in zip(outs, wanted):
            for d in range(4):
                for i, e in enumerate(zs):
                    to = pl.ds((d * len(zs) + i) * W, W)
                    copy = pltpu.make_async_copy(g.at[:, pl.ds(column(d, e, flip, place), W)], out.at[:, to], sem.at[len(copies)])
                    copy.start()
                    copies.append(copy)
        for copy in copies:
            copy.wait()

    return pl.pallas_call(
        body,
        out_shape=tuple(jax.ShapeDtypeStruct((W, 4 * len(zs) * W), jnp.bfloat16) for zs, _ in wanted),
        in_specs=[HB] + [ANY] * len(after),
        out_specs=(VM,) * len(wanted),
        scratch_shapes=[pltpu.SemaphoreType.DMA((4 * sum(len(zs) for zs, _ in wanted),))],
        compiler_params=params(8),
        name="pick_out",
    )(grad, *after)


def pair_sums(mine, other, zs, groups, after=()):
    m = len(zs)

    def body(g, o, *refs):
        own, *codes = refs[len(after) :]
        for d in (2, 1, 3, 0):
            for i, e in enumerate(zs):
                at = pl.ds((d * m + i) * W, W)
                total = g[:, at].astype(jnp.float32) + o[:, at].astype(jnp.float32)
                if d == 0:
                    own[:, i * W : (i + 1) * W] = total
                else:
                    q = [e in group for group in groups].index(True)
                    ref = codes[q * 3 + d - 1]
                    to = pl.ds(groups[q].index(e) * W, W)
                    code, scale = encode(total, PAIR_BOUND)
                    ref[0:W, to] = code
                    ref[W : W + EXTRA, to] = scale

    sent = [jax.ShapeDtypeStruct((W + EXTRA, len(group) * W), jnp.int16) for group in groups for _ in range(3)]
    return pl.pallas_call(
        body,
        out_shape=(jax.ShapeDtypeStruct((W, m * W), jnp.float32), *sent),
        in_specs=[VM, VM] + [ANY] * len(after),
        out_specs=(VM,) * (1 + len(sent)),
        compiler_params=params(12),
        name="pair_sums",
    )(mine, other, *after)


def octet_sums(own, got, after=()):
    m = got[0].shape[1] // W

    def body(own, g1, g2, g3, *refs):
        outs = refs[len(after) :]
        for i in range(m):
            at = pl.ds(i * W, W)
            total = own[:, at]
            for ref in (g1, g2, g3):
                total = total + decode(ref[0:W, at], ref[W : W + 1, at], PAIR_BOUND)
            code, scale = encode(total, OCTET_BOUND)
            outs[i][0:W, :] = code
            outs[i][W : W + EXTRA, :] = scale

    return pl.pallas_call(
        body,
        out_shape=(jax.ShapeDtypeStruct((W + EXTRA, W), jnp.int16),) * m,
        in_specs=[VM] * 4 + [ANY] * len(after),
        out_specs=(VM,) * m,
        compiler_params=params(12),
        name="octet_sums",
    )(own, *got, *after)


def dot(a, b, dims=((1,), (0,)), precision=None):
    return lax.dot_general(a, b, (dims, ((), ())), precision=precision, preferred_element_type=jnp.float32)


def thirds(value):
    first = value.astype(jnp.bfloat16)
    rest = value - first.astype(jnp.float32)
    second = rest.astype(jnp.bfloat16)
    third = (rest - second.astype(jnp.float32)).astype(jnp.bfloat16)
    return first, second, third


def own_masks(ids):
    lane = lax.broadcasted_iota(jnp.int32, (1, 512), 1)
    down = lax.broadcasted_iota(jnp.int32, (W, 512), 0)
    row = (lane >> 7) * BLOCK + (ids >> 6)
    col = ((lane >> 5) & 3) * BLOCK + (ids & 63)
    return down == row, down == col


def transform(own, along_x, along_z, momentum, table, ids):
    def body(own, x1, x2, x3, z1, z2, z3, mom, table, ids, acc_out, coeff_out, note_out):
        total = own[:, W : 2 * W]
        for ref in (x1, x2, x3):
            total = total + decode(ref[0:W, :], ref[W : W + 1, :], PAIR_BOUND)
        for ref in (z1, z2, z3):
            total = total + decode(ref[0:W, :], ref[W : W + 1, :], OCTET_BOUND)
        acc = DECAY * mom[...] + total
        acc_out[...] = acc
        t = table[...]
        coeffs = dot(dot(t, acc, precision=HI), t, ((1,), (1,)), HI)
        coeff_out[...] = coeffs
        rows, cols = own_masks(ids[...])
        chosen = cols.astype(jnp.float32).astype(jnp.bfloat16)
        parts = thirds(coeffs)
        spread = dot(parts[0], chosen) + (dot(parts[1], chosen) + dot(parts[2], chosen))
        note_out[:, 0:512] = jnp.sum(jnp.where(rows, spread, 0.0), axis=0, keepdims=True)
        note_out[:, 512:1024] = ids[...].astype(jnp.float32)

    return pl.pallas_call(
        body,
        out_shape=(
            jax.ShapeDtypeStruct((W, W), jnp.float32),
            jax.ShapeDtypeStruct((W, W), jnp.float32),
            jax.ShapeDtypeStruct((1, 1024), jnp.float32),
        ),
        in_specs=[VM] * 10,
        out_specs=(VM, VM, VM),
        compiler_params=params(16),
        name="transform",
    )(own, *along_x, *along_z, momentum, table, ids)


def momentum_step(acc, coeffs, table, ids):
    def body(acc, coeffs, table, ids, out):
        rows, cols = own_masks(ids[...])
        mask = dot(rows.astype(jnp.float32).astype(jnp.bfloat16), cols.astype(jnp.float32).astype(jnp.bfloat16), ((1,), (1,)))
        dense = jnp.where(mask > 0.5, coeffs[...], 0.0)
        t = table[...]
        out[...] = acc[...] - dot(dot(t, dense, ((0,), (0,)), HI), t, precision=HI)

    return pl.pallas_call(
        body,
        out_shape=jax.ShapeDtypeStruct((W, W), jnp.float32),
        in_specs=[VM] * 4,
        out_specs=VM,
        compiler_params=params(16),
        cost_estimate=pl.CostEstimate(flops=10**9, transcendentals=0, bytes_accessed=10**6),
        name="momentum_step",
    )(acc, coeffs, table, ids)


def bundle(parts, flat=False):
    shape = parts[0].shape
    out_shape = (len(parts),) + (shape[1:] if flat else shape)

    def body(*refs):
        out = refs[-1]
        for i in range(len(parts)):
            if flat:
                out[i : i + 1, :] = refs[i][...]
            else:
                out[i] = refs[i][...]

    return pl.pallas_call(
        body,
        out_shape=jax.ShapeDtypeStruct(out_shape, parts[0].dtype),
        in_specs=[VM] * len(parts),
        out_specs=VM,
        compiler_params=params(8),
        name="bundle",
    )(*parts)


def master_step(master, table, near, far):
    def body(master, table, near, far, out, low):
        me = lax.axis_index("group")
        notes = [near[i : i + 1, :] for i in range(4)] + [far[i : i + 1, :] for i in range(4)]
        ordered = []
        for g in range(8):
            rel = me ^ g
            found = notes[0]
            for r in range(1, 8):
                found = jnp.where(rel == r, notes[r], found)
            ordered.append(found)
        bands = []
        for a in range(4):
            v = jnp.concatenate([x[:, a * 128 : a * 128 + 128] for x in ordered], axis=1)
            k = jnp.concatenate([x[:, 512 + a * 128 : 640 + a * 128] for x in ordered], axis=1).astype(jnp.int32)
            lane = lax.broadcasted_iota(jnp.int32, (1, 1024), 1)
            row = lax.broadcasted_iota(jnp.int32, (BLOCK, 1024), 0) == (k >> 6)
            col = lax.broadcasted_iota(jnp.int32, (W, 1024), 0) == (((lane >> 5) & 3) * BLOCK + (k & 63))
            col = col.astype(jnp.float32).astype(jnp.bfloat16)
            stack = jnp.concatenate([jnp.where(row, p.astype(jnp.float32), 0.0).astype(jnp.bfloat16) for p in thirds(v)], axis=0)
            both = dot(stack, col, ((1,), (1,)))
            bands.append(both[0:BLOCK] + (both[BLOCK : 2 * BLOCK] + both[2 * BLOCK :]))
        union = jnp.concatenate(bands, axis=0)
        t = table[...]
        change = dot(dot(t, union, ((0,), (0,)), HI), t, precision=HI)
        result = master[...] - STEP * jnp.tanh(change)
        out[...] = result
        low[...] = result.astype(jnp.bfloat16)

    return pl.pallas_call(
        body,
        out_shape=(jax.ShapeDtypeStruct((W, W), jnp.float32), jax.ShapeDtypeStruct((W, W), jnp.bfloat16)),
        in_specs=[VM] * 4,
        out_specs=(VM, VM),
        compiler_params=params(16),
        name="master_step",
    )(master, table, near, far)


def joined(stacks, keys, whole=None):
    count = sum(len(k) for k in keys)

    def body(*refs):
        out, sem = refs[-2:]
        place = own_place()
        copies = []
        for ref, places in zip(refs, keys):
            for i, key in enumerate(places):
                source = ref.at[i] if len(places) > 1 else ref
                copy = pltpu.make_async_copy(source, out.at[:, pl.ds(column(*key, place), W)], sem.at[len(copies)])
                copy.start()
                copies.append(copy)
        for copy in copies:
            copy.wait()

    more = () if whole is None else (whole,)
    return pl.pallas_call(
        body,
        out_shape=jax.ShapeDtypeStruct((W, 32 * W), jnp.bfloat16),
        in_specs=[VM] * len(stacks) + [ANY] * len(more),
        out_specs=ANY,
        input_output_aliases={len(stacks): 0} if more else {},
        scratch_shapes=[pltpu.SemaphoreType.DMA((count,))],
        compiler_params=params(12),
        name="joined",
    )(*stacks, *more)


NEXT = (2, 1, 3)


def step(gradients, momentum, master, indices):
    table = jnp.asarray(cosine_blocks())
    grad = pltpu.with_memory_space_constraint(gradients[0, 0], pltpu.HBM)
    ids = indices[0].reshape(1, 512)

    far, near = (2, 3), (1, 0)
    (given_far,) = pick_out(grad, ((far, 1),))
    mine_far, given_near, mine_near = pick_out(grad, ((far, 0), (near, 1), (near, 0)), (given_far,))
    own_far, *codes_far = pair_sums(mine_far, swapped(given_far, "c", 1), far, (far,))
    got_far = {d: swapped(codes_far[d - 1], "x", d) for d in NEXT}
    own_near, *codes_near = pair_sums(mine_near, swapped(given_near, "c", 1), near, ((1,), (0,)), (own_far,))
    got_mid = {d: swapped(codes_near[d - 1], "x", d) for d in NEXT}
    got_own = {d: swapped(codes_near[d + 2], "x", d) for d in NEXT}
    out2, out3 = octet_sums(own_far, [got_far[d] for d in (1, 2, 3)])
    in2, in3 = swapped(out2, "z", 2), swapped(out3, "z", 3)
    (out1,) = octet_sums(own_near, [got_mid[d] for d in (1, 2, 3)], (out2,))
    in1 = swapped(out1, "z", 1)

    acc, coeffs, note = transform(own_near, [got_own[d] for d in (1, 2, 3)], (in1, in2, in3), momentum[0], table, ids)
    notes = [note] + [swapped(note, "group", r) for r in (1, 2, 3)]
    momentum_out = momentum_step(acc, coeffs, table, ids)
    mine = bundle(notes, flat=True)
    theirs = swapped(mine, "group", 4)
    master_out, low = master_step(master, table, mine, theirs)

    by_z = [low] + [swapped(low, "z", e) for e in (1, 2, 3)]
    by_x = {(d, e): swapped(by_z[e], "x", d) for e in range(4) for d in NEXT}
    parts = {
        "early": [(0, e) for e in range(4)] + [(d, e) for e in (0, 1) for d in NEXT],
        "mid": [(d, 2) for d in NEXT],
        "late": [(d, 3) for d in NEXT],
    }
    by_x.update({(0, e): by_z[e] for e in range(4)})
    whole = None
    for keys in parts.values():
        half = bundle([by_x[key] for key in keys])
        other = swapped(half, "c", 1)
        whole = joined([half, other], [[(*key, f) for key in keys] for f in (0, 1)], whole)
    params_full = whole
    return momentum_out[None], master_out, params_full


def solution(mesh):
    torus = Mesh(mesh.devices.reshape(mesh.shape["group"], 4, 4, 2), ("group", "x", "z", "c"))
    return jax.shard_map(
        step,
        mesh=torus,
        in_specs=(P("group", SHARD, None, None), P("group", None, SHARD), P(None, SHARD), P("group", None, SHARD, None)),
        out_specs=(P("group", None, SHARD), P(None, SHARD), P()),
        check_vma=False,
    )
```

profile of v0, /device:TPU:1, one launch (start us, length us, event | category | flops | bytes accessed | tf_op | source)
XLA Modules:
  0.0 106.1 jit_solution(2994824748431295649)
XLA Ops:
  2.0 3.3 %collective-permute-start.1 = (bf16[256,2048]{1,0:T(8,128)(2,1)S(1)}, bf16[256,2048]{1,0:T(8,128)(2,1)S(1)}, u32[]{:S(2)}, u32[]{:S(2)}) collective-permute-start(bf16[256,2048]{1,0:T(8,128)(2,1)S(1)} %pick_out.2.refs_0_), channel_id=1, source_target_pairs={{0,1},{1,0},{2,3},{3,2},{4,5},{5,4},{6,7},{7,6},{8,9},{9,8},{10,11... | collective-permute-start | bytes 3145736 | tf_op jit(solution)/shard_map/ppermute | solution.py:32
  5.3 2.2 %pick_out.3 = (bf16[256,2048]{1,0:T(8,128)(2,1)S(1)}, bf16[256,2048]{1,0:T(8,128)(2,1)S(1)}, bf16[256,2048]{1,0:T(8,128)(2,1)S(1)}) custom-call(bf16[256,8192]{1,0:T(8,128)(2,1)} %bitcast.5, bf16[256,2048]{1,0:T(8,128)(2,1)S(1)} %pick_out.2.refs_0_), custom_call_target="tpu_custom_call" | custom-call | tf_op jit(solution)/shard_map/pick_out/pallas_call | solution.py:79
  9.0 3.1 %collective-permute-start.9 = (s16[264,512]{1,0:T(8,128)(2,1)S(1)}, s16[264,512]{1,0:T(8,128)(2,1)S(1)}, u32[]{:S(2)}, u32[]{:S(2)}) collective-permute-start(s16[264,512]{1,0:T(8,128)(2,1)S(1)} %get-tuple-element.36), channel_id=1, source_target_pairs={{0,16},{8,24},{16,0},{24,8},{1,17},{9,25},{17,1},{25,9},{2,18},{10... | collective-permute-start | bytes 811016 | tf_op jit(solution)/shard_map/ppermute | solution.py:32
  12.6 1.9 %collective-permute-start.6 = (s16[264,256]{1,0:T(8,128)(2,1)S(1)}, s16[264,256]{1,0:T(8,128)(2,1)S(1)}, u32[]{:S(2)}, u32[]{:S(2)}) collective-permute-start(s16[264,256]{1,0:T(8,128)(2,1)S(1)} %get-tuple-element.33), channel_id=1, source_target_pairs={{0,16},{8,24},{16,0},{24,8},{1,17},{9,25},{17,1},{25,9},{2,18},{10... | collective-permute-start | bytes 405512 | tf_op jit(solution)/shard_map/ppermute | solution.py:32
  14.5 2.4 %collective-permute-done.10.g3 = s16[264,512]{1,0:T(8,128)(2,1)S(1)} collective-permute-done((s16[264,512]{1,0:T(8,128)(2,1)S(1)}, s16[264,512]{1,0:T(8,128)(2,1)S(1)}, u32[]{:S(2)}, u32[]{:S(2)}) %collective-permute-start.10) | collective-permute-done | bytes 270368 | tf_op jit(solution)/shard_map/ppermute | solution.py:32
  17.7 6.0 %collective-permute-done.9.g2 = s16[264,512]{1,0:T(8,128)(2,1)S(1)} collective-permute-done((s16[264,512]{1,0:T(8,128)(2,1)S(1)}, s16[264,512]{1,0:T(8,128)(2,1)S(1)}, u32[]{:S(2)}, u32[]{:S(2)}) %collective-permute-start.9) | collective-permute-done | bytes 270368 | tf_op jit(solution)/shard_map/ppermute | solution.py:32
  26.9 2.6 %collective-permute-done.6.g2 = s16[264,256]{1,0:T(8,128)(2,1)S(1)} collective-permute-done((s16[264,256]{1,0:T(8,128)(2,1)S(1)}, s16[264,256]{1,0:T(8,128)(2,1)S(1)}, u32[]{:S(2)}, u32[]{:S(2)}) %collective-permute-start.6) | collective-permute-done | bytes 135200 | tf_op jit(solution)/shard_map/ppermute | solution.py:32
  32.7 2.4 %collective-permute-start.13 = (s16[264,256]{1,0:T(8,128)(2,1)S(1)}, s16[264,256]{1,0:T(8,128)(2,1)S(1)}, u32[]{:S(2)}, u32[]{:S(2)}) collective-permute-start(s16[264,256]{1,0:T(8,128)(2,1)S(1)} %get-tuple-element.39), channel_id=1, source_target_pairs={{0,6},{2,4},{4,2},{6,0},{1,7},{3,5},{5,3},{7,1},{8,14},{10,12},{12... | collective-permute-start | bytes 405512 | tf_op jit(solution)/shard_map/ppermute | solution.py:32
  36.5 3.3 %collective-permute-done.13.z3 = s16[264,256]{1,0:T(8,128)(2,1)S(1)} collective-permute-done((s16[264,256]{1,0:T(8,128)(2,1)S(1)}, s16[264,256]{1,0:T(8,128)(2,1)S(1)}, u32[]{:S(2)}, u32[]{:S(2)}) %collective-permute-start.13) | collective-permute-done | bytes 135200 | tf_op jit(solution)/shard_map/ppermute | solution.py:32
  42.8 2.6 %collective-permute-start.15 = (f32[1,1024]{1,0:T(1,128)S(1)}, f32[1,1024]{1,0:T(1,128)S(1)}, u32[]{:S(2)}, u32[]{:S(2)}) collective-permute-start(f32[1,1024]{1,0:T(1,128)S(1)} %get-tuple-element.42.refs_0_), channel_id=1, source_target_pairs={{0,64},{32,96},{64,0},{96,32},{128,192},{160,224},{192,128},{224,1... | collective-permute-start | bytes 12296 | tf_op jit(solution)/shard_map/ppermute | solution.py:32
  46.8 2.3 %collective-permute-done.16.refs_3_ = f32[1,1024]{1,0:T(1,128)S(1)} collective-permute-done((f32[1,1024]{1,0:T(1,128)S(1)}, f32[1,1024]{1,0:T(1,128)S(1)}, u32[]{:S(2)}, u32[]{:S(2)}) %collective-permute-start.16) | collective-permute-done | bytes 4128 | tf_op jit(solution)/shard_map/ppermute | solution.py:32
  49.1 5.0 %collective-permute-start.17 = (f32[4,1024]{1,0:T(4,128)S(1)}, f32[4,1024]{1,0:T(4,128)S(1)}, u32[]{:S(2)}, u32[]{:S(2)}) collective-permute-start(f32[4,1024]{1,0:T(4,128)S(1)} %bundle.4.near), channel_id=1, source_target_pairs={{0,128},{32,160},{64,192},{96,224},{128,0},{160,32},{192,64},{224,... | collective-permute-start | bytes 49160 | tf_op jit(solution)/shard_map/ppermute | solution.py:32
  55.6 2.6 %master_step.1 = (f32[256,256]{1,0:T(8,128)}, bf16[256,256]{1,0:T(8,128)(2,1)S(1)}) custom-call(f32[256,256]{1,0:T(8,128)S(1)} %copy-done.1, f32[256,256]{1,0:T(8,128)S(1)} %copy-done, f32[4,1024]{1,0:T(4,128)S(1)} %bundle.4.near, f32[4,1024]{1,0:T(4,128)S(1)} %collective-permute-done.17.far), custom_call_target="tpu_custom_call" | custom-call | tf_op jit(solution)/shard_map/master_step/pallas_call | solution.py:267
  58.2 2.9 %collective-permute-start.28 = (bf16[256,256]{1,0:T(8,128)(2,1)S(1)}, bf16[256,256]{1,0:T(8,128)(2,1)S(1)}, u32[]{:S(2)}, u32[]{:S(2)}) collective-permute-start(bf16[256,256]{1,0:T(8,128)(2,1)S(1)} %get-tuple-element.44.refs_0_), channel_id=1, source_target_pairs={{0,2},{2,0},{4,6},{6,4},{1,3},{3,1},{5,7},{7,5},{8,10},{10,8},{12,... | collective-permute-start | bytes 393224 | tf_op jit(solution)/shard_map/ppermute | solution.py:32
  61.1 2.2 %collective-permute-start.18 = (bf16[256,256]{1,0:T(8,128)(2,1)S(1)}, bf16[256,256]{1,0:T(8,128)(2,1)S(1)}, u32[]{:S(2)}, u32[]{:S(2)}) collective-permute-start(bf16[256,256]{1,0:T(8,128)(2,1)S(1)} %get-tuple-element.44.refs_0_), channel_id=1, source_target_pairs={{0,6},{2,4},{4,2},{6,0},{1,7},{3,5},{5,3},{7,1},{8,14},{10,12},{12... | collective-permute-start | bytes 393224 | tf_op jit(solution)/shard_map/ppermute | solution.py:32
  68.7 2.1 %collective-permute-done.23.refs_2_ = bf16[256,256]{1,0:T(8,128)(2,1)S(1)} collective-permute-done((bf16[256,256]{1,0:T(8,128)(2,1)S(1)}, bf16[256,256]{1,0:T(8,128)(2,1)S(1)}, u32[]{:S(2)}, u32[]{:S(2)}) %collective-permute-start.23) | collective-permute-done | bytes 131104 | tf_op jit(solution)/shard_map/ppermute | solution.py:32
  70.9 2.5 %collective-permute-start.34 = (bf16[256,256]{1,0:T(8,128)(2,1)S(1)}, bf16[256,256]{1,0:T(8,128)(2,1)S(1)}, u32[]{:S(2)}, u32[]{:S(2)}) collective-permute-start(bf16[256,256]{1,0:T(8,128)(2,1)S(1)} %collective-permute-done.28.refs_1_), channel_id=1, source_target_pairs={{0,24},{8,16},{16,8},{24,0},{1,25},{9,17},{17,9},{25,1},{2,26},{10... | collective-permute-start | bytes 393224 | tf_op jit(solution)/shard_map/ppermute | solution.py:32
  73.4 2.5 %collective-permute-done.33.refs_8_ = bf16[256,256]{1,0:T(8,128)(2,1)S(1)} collective-permute-done((bf16[256,256]{1,0:T(8,128)(2,1)S(1)}, bf16[256,256]{1,0:T(8,128)(2,1)S(1)}, u32[]{:S(2)}, u32[]{:S(2)}) %collective-permute-start.33) | collective-permute-done | bytes 131104 | tf_op jit(solution)/shard_map/ppermute | solution.py:32
  77.7 6.0 %collective-permute-start.35 = (bf16[10,256,256]{2,1,0:T(8,128)(2,1)S(1)}, bf16[10,256,256]{2,1,0:T(8,128)(2,1)S(1)}, u32[]{:S(2)}, u32[]{:S(2)}) collective-permute-start(bf16[10,256,256]{2,1,0:T(8,128)(2,1)S(1)} %bundle.7.refs_0_), channel_id=1, source_target_pairs={{0,1},{1,0},{2,3},{3,2},{4,5},{5,4},{6,7},{7,6},{8,9},{9,8},{10,11... | collective-permute-start | bytes 3932168 | tf_op jit(solution)/shard_map/ppermute | solution.py:32
  83.7 1.9 %collective-permute-start.24 = (bf16[256,256]{1,0:T(8,128)(2,1)S(1)}, bf16[256,256]{1,0:T(8,128)(2,1)S(1)}, u32[]{:S(2)}, u32[]{:S(2)}) collective-permute-start(bf16[256,256]{1,0:T(8,128)(2,1)S(1)} %collective-permute-done.23.refs_2_), channel_id=1, source_target_pairs={{0,16},{8,24},{16,0},{24,8},{1,17},{9,25},{17,1},{25,9},{2,18},{10... | collective-permute-start | bytes 393224 | tf_op jit(solution)/shard_map/ppermute | solution.py:32
  90.2 2.4 %collective-permute-done.25.refs_1_ = bf16[256,256]{1,0:T(8,128)(2,1)S(1)} collective-permute-done((bf16[256,256]{1,0:T(8,128)(2,1)S(1)}, bf16[256,256]{1,0:T(8,128)(2,1)S(1)}, u32[]{:S(2)}, u32[]{:S(2)}) %collective-permute-start.25) | collective-permute-done | bytes 131104 | tf_op jit(solution)/shard_map/ppermute | solution.py:32
  95.8 2.4 %collective-permute-done.20.refs_1_ = bf16[256,256]{1,0:T(8,128)(2,1)S(1)} collective-permute-done((bf16[256,256]{1,0:T(8,128)(2,1)S(1)}, bf16[256,256]{1,0:T(8,128)(2,1)S(1)}, u32[]{:S(2)}, u32[]{:S(2)}) %collective-permute-start.20) | collective-permute-done | bytes 131104 | tf_op jit(solution)/shard_map/ppermute | solution.py:32
  98.2 2.2 %collective-permute-start.22 = (bf16[3,256,256]{2,1,0:T(8,128)(2,1)S(1)}, bf16[3,256,256]{2,1,0:T(8,128)(2,1)S(1)}, u32[]{:S(2)}, u32[]{:S(2)}) collective-permute-start(bf16[3,256,256]{2,1,0:T(8,128)(2,1)S(1)} %bundle.5.refs_0_), channel_id=1, source_target_pairs={{0,1},{1,0},{2,3},{3,2},{4,5},{5,4},{6,7},{7,6},{8,9},{9,8},{10,11... | collective-permute-start | bytes 1179656 | tf_op jit(solution)/shard_map/ppermute | solution.py:32
  100.3 2.0 %momentum_step.1 = f32[256,256]{1,0:T(8,128)} custom-call(f32[256,256]{1,0:T(8,128)S(1)} %get-tuple-element.40.acc, f32[256,256]{1,0:T(8,128)S(1)} %get-tuple-element.41.coeffs, f32[256,256]{1,0:T(8,128)S(1)} %copy-done, s32[1,512]{1,0:T(1,128)S(1)} %reshape_squeeze.3.ids), custom_call_target="tpu_custom_call" | custom-call | flops 1000000000 | bytes 1000000 | tf_op jit(solution)/shard_map/momentum_step/pallas_call | solution.py:205
  (73 shorter events, 36.3 us)
Async XLA Ops:
  8.1 8.9 %collective-permute-start.10 = (s16[264,512]{1,0:T(8,128)(2,1)S(1)}, s16[264,512]{1,0:T(8,128)(2,1)S(1)}, u32[]{:S(2)}, u32[]{:S(2)}) collective-permute-start(s16[264,512]{1,0:T(8,128)(2,1)S(1)} %get-tuple-element.37), channel_id=1, source_target_pairs={{0,24},{8,16},{16,8},{24,0},{1,25},{9,17},{17,9},{25,1},{2,26},{10... | collective-permute-start | bytes 811016 | tf_op jit(solution)/shard_map/ppermute | solution.py:32
  9.0 8.8 %collective-permute-start.8 = (s16[264,512]{1,0:T(8,128)(2,1)S(1)}, s16[264,512]{1,0:T(8,128)(2,1)S(1)}, u32[]{:S(2)}, u32[]{:S(2)}) collective-permute-start(s16[264,512]{1,0:T(8,128)(2,1)S(1)} %get-tuple-element.35), channel_id=1, source_target_pairs={{0,8},{8,0},{16,24},{24,16},{1,9},{9,1},{17,25},{25,17},{2,10},{10... | collective-permute-start | bytes 811016 | tf_op jit(solution)/shard_map/ppermute | solution.py:32
  9.0 14.7 %collective-permute-start.9 = (s16[264,512]{1,0:T(8,128)(2,1)S(1)}, s16[264,512]{1,0:T(8,128)(2,1)S(1)}, u32[]{:S(2)}, u32[]{:S(2)}) collective-permute-start(s16[264,512]{1,0:T(8,128)(2,1)S(1)} %get-tuple-element.36), channel_id=1, source_target_pairs={{0,16},{8,24},{16,0},{24,8},{1,17},{9,25},{17,1},{25,9},{2,18},{10... | collective-permute-start | bytes 811016 | tf_op jit(solution)/shard_map/ppermute | solution.py:32
  12.5 12.5 %collective-permute-start.5 = (s16[264,256]{1,0:T(8,128)(2,1)S(1)}, s16[264,256]{1,0:T(8,128)(2,1)S(1)}, u32[]{:S(2)}, u32[]{:S(2)}) collective-permute-start(s16[264,256]{1,0:T(8,128)(2,1)S(1)} %get-tuple-element.32), channel_id=1, source_target_pairs={{0,8},{8,0},{16,24},{24,16},{1,9},{9,1},{17,25},{25,17},{2,10},{10... | collective-permute-start | bytes 405512 | tf_op jit(solution)/shard_map/ppermute | solution.py:32
  12.6 16.9 %collective-permute-start.6 = (s16[264,256]{1,0:T(8,128)(2,1)S(1)}, s16[264,256]{1,0:T(8,128)(2,1)S(1)}, u32[]{:S(2)}, u32[]{:S(2)}) collective-permute-start(s16[264,256]{1,0:T(8,128)(2,1)S(1)} %get-tuple-element.33), channel_id=1, source_target_pairs={{0,16},{8,24},{16,0},{24,8},{1,17},{9,25},{17,1},{25,9},{2,18},{10... | collective-permute-start | bytes 405512 | tf_op jit(solution)/shard_map/ppermute | solution.py:32
  17.0 13.8 %collective-permute-start.7 = (s16[264,256]{1,0:T(8,128)(2,1)S(1)}, s16[264,256]{1,0:T(8,128)(2,1)S(1)}, u32[]{:S(2)}, u32[]{:S(2)}) collective-permute-start(s16[264,256]{1,0:T(8,128)(2,1)S(1)} %get-tuple-element.34), channel_id=1, source_target_pairs={{0,24},{8,16},{16,8},{24,0},{1,25},{9,17},{17,9},{25,1},{2,26},{10... | collective-permute-start | bytes 405512 | tf_op jit(solution)/shard_map/ppermute | solution.py:32
  17.7 14.9 %collective-permute-start.2 = (s16[264,256]{1,0:T(8,128)(2,1)S(1)}, s16[264,256]{1,0:T(8,128)(2,1)S(1)}, u32[]{:S(2)}, u32[]{:S(2)}) collective-permute-start(s16[264,256]{1,0:T(8,128)(2,1)S(1)} %get-tuple-element.29), channel_id=1, source_target_pairs={{0,8},{8,0},{16,24},{24,16},{1,9},{9,1},{17,25},{25,17},{2,10},{10... | collective-permute-start | bytes 405512 | tf_op jit(solution)/shard_map/ppermute | solution.py:32
  23.7 11.6 %collective-permute-start.3 = (s16[264,256]{1,0:T(8,128)(2,1)S(1)}, s16[264,256]{1,0:T(8,128)(2,1)S(1)}, u32[]{:S(2)}, u32[]{:S(2)}) collective-permute-start(s16[264,256]{1,0:T(8,128)(2,1)S(1)} %get-tuple-element.30), channel_id=1, source_target_pairs={{0,16},{8,24},{16,0},{24,8},{1,17},{9,25},{17,1},{25,9},{2,18},{10... | collective-permute-start | bytes 405512 | tf_op jit(solution)/shard_map/ppermute | solution.py:32
  25.0 10.3 %collective-permute-start.4 = (s16[264,256]{1,0:T(8,128)(2,1)S(1)}, s16[264,256]{1,0:T(8,128)(2,1)S(1)}, u32[]{:S(2)}, u32[]{:S(2)}) collective-permute-start(s16[264,256]{1,0:T(8,128)(2,1)S(1)} %get-tuple-element.31), channel_id=1, source_target_pairs={{0,24},{8,16},{16,8},{24,0},{1,25},{9,17},{17,9},{25,1},{2,26},{10... | collective-permute-start | bytes 405512 | tf_op jit(solution)/shard_map/ppermute | solution.py:32
  29.5 7.0 %collective-permute-start.12 = (s16[264,256]{1,0:T(8,128)(2,1)S(1)}, s16[264,256]{1,0:T(8,128)(2,1)S(1)}, u32[]{:S(2)}, u32[]{:S(2)}) collective-permute-start(s16[264,256]{1,0:T(8,128)(2,1)S(1)} %get-tuple-element.38.refs_0_), channel_id=1, source_target_pairs={{0,4},{2,6},{4,0},{6,2},{1,5},{3,7},{5,1},{7,3},{8,12},{10,14},{12... | collective-permute-start | bytes 405512 | tf_op jit(solution)/shard_map/ppermute | solution.py:32
  32.7 7.2 %collective-permute-start.13 = (s16[264,256]{1,0:T(8,128)(2,1)S(1)}, s16[264,256]{1,0:T(8,128)(2,1)S(1)}, u32[]{:S(2)}, u32[]{:S(2)}) collective-permute-start(s16[264,256]{1,0:T(8,128)(2,1)S(1)} %get-tuple-element.39), channel_id=1, source_target_pairs={{0,6},{2,4},{4,2},{6,0},{1,7},{3,5},{5,3},{7,1},{8,14},{10,12},{12... | collective-permute-start | bytes 405512 | tf_op jit(solution)/shard_map/ppermute | solution.py:32
  58.2 8.1 %collective-permute-start.28 = (bf16[256,256]{1,0:T(8,128)(2,1)S(1)}, bf16[256,256]{1,0:T(8,128)(2,1)S(1)}, u32[]{:S(2)}, u32[]{:S(2)}) collective-permute-start(bf16[256,256]{1,0:T(8,128)(2,1)S(1)} %get-tuple-element.44.refs_0_), channel_id=1, source_target_pairs={{0,2},{2,0},{4,6},{6,4},{1,3},{3,1},{5,7},{7,5},{8,10},{10,8},{12,... | collective-permute-start | bytes 393224 | tf_op jit(solution)/shard_map/ppermute | solution.py:32
  63.3 7.6 %collective-permute-start.23 = (bf16[256,256]{1,0:T(8,128)(2,1)S(1)}, bf16[256,256]{1,0:T(8,128)(2,1)S(1)}, u32[]{:S(2)}, u32[]{:S(2)}) collective-permute-start(bf16[256,256]{1,0:T(8,128)(2,1)S(1)} %get-tuple-element.44.refs_0_), channel_id=1, source_target_pairs={{0,4},{2,6},{4,0},{6,2},{1,5},{3,7},{5,1},{7,3},{8,12},{10,14},{12... | collective-permute-start | bytes 393224 | tf_op jit(solution)/shard_map/ppermute | solution.py:32
  63.3 7.6 %collective-permute-start.29 = (bf16[256,256]{1,0:T(8,128)(2,1)S(1)}, bf16[256,256]{1,0:T(8,128)(2,1)S(1)}, u32[]{:S(2)}, u32[]{:S(2)}) collective-permute-start(bf16[256,256]{1,0:T(8,128)(2,1)S(1)} %get-tuple-element.44.refs_0_), channel_id=1, source_target_pairs={{0,16},{8,24},{16,0},{24,8},{1,17},{9,25},{17,1},{25,9},{2,18},{10... | collective-permute-start | bytes 393224 | tf_op jit(solution)/shard_map/ppermute | solution.py:32
  64.9 8.4 %collective-permute-start.30 = (bf16[256,256]{1,0:T(8,128)(2,1)S(1)}, bf16[256,256]{1,0:T(8,128)(2,1)S(1)}, u32[]{:S(2)}, u32[]{:S(2)}) collective-permute-start(bf16[256,256]{1,0:T(8,128)(2,1)S(1)} %get-tuple-element.44.refs_0_), channel_id=1, source_target_pairs={{0,8},{8,0},{16,24},{24,16},{1,9},{9,1},{17,25},{25,17},{2,10},{10... | collective-permute-start | bytes 393224 | tf_op jit(solution)/shard_map/ppermute | solution.py:32
  66.3 7.0 %collective-permute-start.31 = (bf16[256,256]{1,0:T(8,128)(2,1)S(1)}, bf16[256,256]{1,0:T(8,128)(2,1)S(1)}, u32[]{:S(2)}, u32[]{:S(2)}) collective-permute-start(bf16[256,256]{1,0:T(8,128)(2,1)S(1)} %get-tuple-element.44.refs_0_), channel_id=1, source_target_pairs={{0,24},{8,16},{16,8},{24,0},{1,25},{9,17},{17,9},{25,1},{2,26},{10... | collective-permute-start | bytes 393224 | tf_op jit(solution)/shard_map/ppermute | solution.py:32
  70.9 6.7 %collective-permute-start.34 = (bf16[256,256]{1,0:T(8,128)(2,1)S(1)}, bf16[256,256]{1,0:T(8,128)(2,1)S(1)}, u32[]{:S(2)}, u32[]{:S(2)}) collective-permute-start(bf16[256,256]{1,0:T(8,128)(2,1)S(1)} %collective-permute-done.28.refs_1_), channel_id=1, source_target_pairs={{0,24},{8,16},{16,8},{24,0},{1,25},{9,17},{17,9},{25,1},{2,26},{10... | collective-permute-start | bytes 393224 | tf_op jit(solution)/shard_map/ppermute | solution.py:32
  77.7 24.7 %collective-permute-start.35 = (bf16[10,256,256]{2,1,0:T(8,128)(2,1)S(1)}, bf16[10,256,256]{2,1,0:T(8,128)(2,1)S(1)}, u32[]{:S(2)}, u32[]{:S(2)}) collective-permute-start(bf16[10,256,256]{2,1,0:T(8,128)(2,1)S(1)} %bundle.7.refs_0_), channel_id=1, source_target_pairs={{0,1},{1,0},{2,3},{3,2},{4,5},{5,4},{6,7},{7,6},{8,9},{9,8},{10,11... | collective-permute-start | bytes 3932168 | tf_op jit(solution)/shard_map/ppermute | solution.py:32
  85.6 6.9 %collective-permute-start.25 = (bf16[256,256]{1,0:T(8,128)(2,1)S(1)}, bf16[256,256]{1,0:T(8,128)(2,1)S(1)}, u32[]{:S(2)}, u32[]{:S(2)}) collective-permute-start(bf16[256,256]{1,0:T(8,128)(2,1)S(1)} %collective-permute-done.23.refs_2_), channel_id=1, source_target_pairs={{0,8},{8,0},{16,24},{24,16},{1,9},{9,1},{17,25},{25,17},{2,10},{10... | collective-permute-start | bytes 393224 | tf_op jit(solution)/shard_map/ppermute | solution.py:32
  86.2 7.0 %collective-permute-start.26 = (bf16[256,256]{1,0:T(8,128)(2,1)S(1)}, bf16[256,256]{1,0:T(8,128)(2,1)S(1)}, u32[]{:S(2)}, u32[]{:S(2)}) collective-permute-start(bf16[256,256]{1,0:T(8,128)(2,1)S(1)} %collective-permute-done.23.refs_2_), channel_id=1, source_target_pairs={{0,24},{8,16},{16,8},{24,0},{1,25},{9,17},{17,9},{25,1},{2,26},{10... | collective-permute-start | bytes 393224 | tf_op jit(solution)/shard_map/ppermute | solution.py:32
  87.0 8.8 %collective-permute-start.19 = (bf16[256,256]{1,0:T(8,128)(2,1)S(1)}, bf16[256,256]{1,0:T(8,128)(2,1)S(1)}, u32[]{:S(2)}, u32[]{:S(2)}) collective-permute-start(bf16[256,256]{1,0:T(8,128)(2,1)S(1)} %collective-permute-done.18.refs_3_), channel_id=1, source_target_pairs={{0,16},{8,24},{16,0},{24,8},{1,17},{9,25},{17,1},{25,9},{2,18},{10... | collective-permute-start | bytes 393224 | tf_op jit(solution)/shard_map/ppermute | solution.py:32
  90.2 8.0 %collective-permute-start.20 = (bf16[256,256]{1,0:T(8,128)(2,1)S(1)}, bf16[256,256]{1,0:T(8,128)(2,1)S(1)}, u32[]{:S(2)}, u32[]{:S(2)}) collective-permute-start(bf16[256,256]{1,0:T(8,128)(2,1)S(1)} %collective-permute-done.18.refs_3_), channel_id=1, source_target_pairs={{0,8},{8,0},{16,24},{24,16},{1,9},{9,1},{17,25},{25,17},{2,10},{10... | collective-permute-start | bytes 393224 | tf_op jit(solution)/shard_map/ppermute | solution.py:32
  93.3 10.7 %collective-permute-start.27 = (bf16[3,256,256]{2,1,0:T(8,128)(2,1)S(1)}, bf16[3,256,256]{2,1,0:T(8,128)(2,1)S(1)}, u32[]{:S(2)}, u32[]{:S(2)}) collective-permute-start(bf16[3,256,256]{2,1,0:T(8,128)(2,1)S(1)} %bundle.6.refs_0_), channel_id=1, source_target_pairs={{0,1},{1,0},{2,3},{3,2},{4,5},{5,4},{6,7},{7,6},{8,9},{9,8},{10,11... | collective-permute-start | bytes 1179656 | tf_op jit(solution)/shard_map/ppermute | solution.py:32
  98.2 6.8 %collective-permute-start.22 = (bf16[3,256,256]{2,1,0:T(8,128)(2,1)S(1)}, bf16[3,256,256]{2,1,0:T(8,128)(2,1)S(1)}, u32[]{:S(2)}, u32[]{:S(2)}) collective-permute-start(bf16[3,256,256]{2,1,0:T(8,128)(2,1)S(1)} %bundle.5.refs_0_), channel_id=1, source_target_pairs={{0,1},{1,0},{2,3},{3,2},{4,5},{5,4},{6,7},{7,6},{8,9},{9,8},{10,11... | collective-permute-start | bytes 1179656 | tf_op jit(solution)/shard_map/ppermute | solution.py:32
  (16 other events, 203.5 us)
where the time goes:
time: 106 us
  starting transfers between devices  55 us (52%)
  waiting for transfers between devices  35.2 us (33%)
  Pallas kernels  14.8 us (14%)
    ppermute x36, starting transfers between devices, swapped(): return lax.ppermute(value, axis, [(i, i ^ mask) for i in range(size)])  55 us
    ppermute x36, waiting for transfers between devices, swapped(): return lax.ppermute(value, axis, [(i, i ^ mask) for i in range(size)])  35.2 us
    pallas_call x2, Pallas kernels, pick_out(): pl.pallas_call(body, out_shape=tuple((jax.ShapeDtypeStruct((W, 4 * len(zs...  3.55 us
    pallas_call x3, Pallas kernels, joined(): pl.pallas_call(body, out_shape=jax.ShapeDtypeStruct((W, 32 * W), jnp.bflo...  3.53 us
    pallas_call x1, Pallas kernels, master_step(): pl.pallas_call(body, out_shape=(jax.ShapeDtypeStruct((W, W), jnp.float32)...  2.62 us
  transfers between devices with their start and end apart: 36, of which 18 were waited for; matrix products, arithmetic and copies ran while one was open for 0% of the time, Pallas kernels for 8%

commit v1 on v0

--- a/solution.py
+++ b/solution.py
@@ -82,31 +82,29 @@
         in_specs=[HB] + [ANY] * len(after),
         out_specs=(VM,) * len(wanted),
         scratch_shapes=[pltpu.SemaphoreType.DMA((4 * sum(len(zs) for zs, _ in wanted),))],
-        compiler_params=params(8),
+        compiler_params=params(12),
         name="pick_out",
     )(grad, *after)
 
 
-def pair_sums(mine, other, zs, groups, after=()):
+def pair_sums(mine, other, zs, after=()):
     m = len(zs)
 
     def body(g, o, *refs):
         own, *codes = refs[len(after) :]
         for d in (2, 1, 3, 0):
-            for i, e in enumerate(zs):
+            for i in range(m):
                 at = pl.ds((d * m + i) * W, W)
                 total = g[:, at].astype(jnp.float32) + o[:, at].astype(jnp.float32)
                 if d == 0:
                     own[:, i * W : (i + 1) * W] = total
                 else:
-                    q = [e in group for group in groups].index(True)
-                    ref = codes[q * 3 + d - 1]
-                    to = pl.ds(groups[q].index(e) * W, W)
+                    ref = codes[i * 3 + d - 1]
                     code, scale = encode(total, PAIR_BOUND)
-                    ref[0:W, to] = code
-                    ref[W : W + EXTRA, to] = scale
-
-    sent = [jax.ShapeDtypeStruct((W + EXTRA, len(group) * W), jnp.int16) for group in groups for _ in range(3)]
+                    ref[0:W, :] = code
+                    ref[W : W + EXTRA, :] = scale
+
+    sent = [jax.ShapeDtypeStruct((W + EXTRA, W), jnp.int16)] * (3 * m)
     return pl.pallas_call(
         body,
         out_shape=(jax.ShapeDtypeStruct((W, m * W), jnp.float32), *sent),
@@ -117,25 +115,21 @@
     )(mine, other, *after)
 
 
-def octet_sums(own, got, after=()):
-    m = got[0].shape[1] // W
-
+def octet_sums(own, first, got, after=()):
     def body(own, g1, g2, g3, *refs):
-        outs = refs[len(after) :]
-        for i in range(m):
-            at = pl.ds(i * W, W)
-            total = own[:, at]
-            for ref in (g1, g2, g3):
-                total = total + decode(ref[0:W, at], ref[W : W + 1, at], PAIR_BOUND)
-            code, scale = encode(total, OCTET_BOUND)
-            outs[i][0:W, :] = code
-            outs[i][W : W + EXTRA, :] = scale
-
-    return pl.pallas_call(
-        body,
-        out_shape=(jax.ShapeDtypeStruct((W + EXTRA, W), jnp.int16),) * m,
+        out = refs[-1]
+        total = own[:, first : first + W]
+        for ref in (g1, g2, g3):
+            total = total + decode(ref[0:W, :], ref[W : W + 1, :], PAIR_BOUND)
+        code, scale = encode(total, OCTET_BOUND)
+        out[0:W, :] = code
+        out[W : W + EXTRA, :] = scale
+
+    return pl.pallas_call(
+        body,
+        out_shape=jax.ShapeDtypeStruct((W + EXTRA, W), jnp.int16),
         in_specs=[VM] * 4 + [ANY] * len(after),
-        out_specs=(VM,) * m,
+        out_specs=VM,
         compiler_params=params(12),
         name="octet_sums",
     )(own, *got, *after)
@@ -163,7 +157,7 @@
 
 def transform(own, along_x, along_z, momentum, table, ids):
     def body(own, x1, x2, x3, z1, z2, z3, mom, table, ids, acc_out, coeff_out, note_out):
-        total = own[:, W : 2 * W]
+        total = own[:, 2 * W : 3 * W]
         for ref in (x1, x2, x3):
             total = total + decode(ref[0:W, :], ref[W : W + 1, :], PAIR_BOUND)
         for ref in (z1, z2, z3):
@@ -311,20 +305,19 @@
     grad = pltpu.with_memory_space_constraint(gradients[0, 0], pltpu.HBM)
     ids = indices[0].reshape(1, 512)
 
-    far, near = (2, 3), (1, 0)
+    far, near = (2,), (3, 1, 0)
     (given_far,) = pick_out(grad, ((far, 1),))
     mine_far, given_near, mine_near = pick_out(grad, ((far, 0), (near, 1), (near, 0)), (given_far,))
-    own_far, *codes_far = pair_sums(mine_far, swapped(given_far, "c", 1), far, (far,))
-    got_far = {d: swapped(codes_far[d - 1], "x", d) for d in NEXT}
-    own_near, *codes_near = pair_sums(mine_near, swapped(given_near, "c", 1), near, ((1,), (0,)), (own_far,))
-    got_mid = {d: swapped(codes_near[d - 1], "x", d) for d in NEXT}
-    got_own = {d: swapped(codes_near[d + 2], "x", d) for d in NEXT}
-    out2, out3 = octet_sums(own_far, [got_far[d] for d in (1, 2, 3)])
-    in2, in3 = swapped(out2, "z", 2), swapped(out3, "z", 3)
-    (out1,) = octet_sums(own_near, [got_mid[d] for d in (1, 2, 3)], (out2,))
-    in1 = swapped(out1, "z", 1)
-
-    acc, coeffs, note = transform(own_near, [got_own[d] for d in (1, 2, 3)], (in1, in2, in3), momentum[0], table, ids)
+    own_far, *codes_far = pair_sums(mine_far, swapped(given_far, "c", 1), far)
+    own_near, *codes_near = pair_sums(mine_near, swapped(given_near, "c", 1), near, (own_far,))
+    codes = {e: part[i * 3 : i * 3 + 3] for part, zs in ((codes_far, far), (codes_near, near)) for i, e in enumerate(zs)}
+    got = {e: [swapped(codes[e][d - 1], "x", d) for d in (1, 2, 3)] for e in (2, 3, 1, 0)}
+    out2 = octet_sums(own_far, 0, got[2])
+    out3 = octet_sums(own_near, 0, got[3], (out2,))
+    out1 = octet_sums(own_near, W, got[1], (out3,))
+    in2, in3, in1 = (swapped(out, "z", e) for e, out in ((2, out2), (3, out3), (1, out1)))
+
+    acc, coeffs, note = transform(own_near, got[0], (in1, in2, in3), momentum[0], table, ids)
     notes = [note] + [swapped(note, "group", r) for r in (1, 2, 3)]
     momentum_out = momentum_step(acc, coeffs, table, ids)
     mine = bundle(notes, flat=True)

time: 106 us -> 110 us (1.038)
  starting transfers between devices: 55 us -> 62.1 us
  waiting for transfers between devices: 35.2 us -> 31.6 us
    ppermute x36 -> x39, starting transfers between devices: 55 us -> 62.1 us  [swapped(): return lax.ppermute(value, axis, [(i, i ^ mask) for i in range(size)])]
    ppermute x36 -> x39, waiting for transfers between devices: 35.2 us -> 31.6 us  [swapped(): return lax.ppermute(value, axis, [(i, i ^ mask) for i in range(size)])]
  transfers between devices with their start and end apart: 36 -> 39, of which waited for: 18 -> 14; matrix products, arithmetic and copies ran while one was open for 0% -> 0% of each run, Pallas kernels for 8% -> 6%
where the time goes in v1:
time: 110 us
  starting transfers between devices  62.1 us (56%)
  waiting for transfers between devices  31.6 us (29%)
  Pallas kernels  14.8 us (13%)
    ppermute x39, starting transfers between devices, swapped(): return lax.ppermute(value, axis, [(i, i ^ mask) for i in range(size)])  62.1 us
    ppermute x39, waiting for transfers between devices, swapped(): return lax.ppermute(value, axis, [(i, i ^ mask) for i in range(size)])  31.6 us
    pallas_call x2, Pallas kernels, pick_out(): pl.pallas_call(body, out_shape=tuple((jax.ShapeDtypeStruct((W, 4 * len(zs...  3.55 us
    pallas_call x3, Pallas kernels, joined(): pl.pallas_call(body, out_shape=jax.ShapeDtypeStruct((W, 32 * W), jnp.bflo...  3.53 us
    pallas_call x1, Pallas kernels, master_step(): pl.pallas_call(body, out_shape=(jax.ShapeDtypeStruct((W, W), jnp.float32)...  2.63 us
  transfers between devices with their start and end apart: 39, of which 14 were waited for; matrix products, arithmetic and copies ran while one was open for 0% of the time, Pallas kernels for 6%

profile of v1, /device:TPU:1, one launch (start us, length us, event | category | flops | bytes accessed | tf_op | source)
XLA Modules:
  0.0 109.7 jit_solution(16738401487325972473)
XLA Ops:
  1.8 2.4 %pick_out.3 = (bf16[256,1024]{1,0:T(8,128)(2,1)S(1)}, bf16[256,3072]{1,0:T(8,128)(2,1)S(1)}, bf16[256,3072]{1,0:T(8,128)(2,1)S(1)}) custom-call(bf16[256,8192]{1,0:T(8,128)(2,1)} %bitcast.5, bf16[256,1024]{1,0:T(8,128)(2,1)S(1)} %pick_out.2.refs_0_), custom_call_target="tpu_custom_call" | custom-call | tf_op jit(solution)/shard_map/pick_out/pallas_call | solution.py:79
  4.2 3.3 %collective-permute-start = (bf16[256,3072]{1,0:T(8,128)(2,1)S(1)}, bf16[256,3072]{1,0:T(8,128)(2,1)S(1)}, u32[]{:S(2)}, u32[]{:S(2)}) collective-permute-start(bf16[256,3072]{1,0:T(8,128)(2,1)S(1)} %get-tuple-element.26), channel_id=1, source_target_pairs={{0,1},{1,0},{2,3},{3,2},{4,5},{5,4},{6,7},{7,6},{8,9},{9,8},{10,11... | collective-permute-start | bytes 4718600 | tf_op jit(solution)/shard_map/ppermute | solution.py:32
  7.6 3.7 %collective-permute-done.1.o = bf16[256,1024]{1,0:T(8,128)(2,1)S(1)} collective-permute-done((bf16[256,1024]{1,0:T(8,128)(2,1)S(1)}, bf16[256,1024]{1,0:T(8,128)(2,1)S(1)}, u32[]{:S(2)}, u32[]{:S(2)}) %collective-permute-start.1) | collective-permute-done | bytes 524320 | tf_op jit(solution)/shard_map/ppermute | solution.py:32
  17.0 3.1 %collective-permute-start.9 = (s16[264,256]{1,0:T(8,128)(2,1)S(1)}, s16[264,256]{1,0:T(8,128)(2,1)S(1)}, u32[]{:S(2)}, u32[]{:S(2)}) collective-permute-start(s16[264,256]{1,0:T(8,128)(2,1)S(1)} %get-tuple-element.37), channel_id=1, source_target_pairs={{0,16},{8,24},{16,0},{24,8},{1,17},{9,25},{17,1},{25,9},{2,18},{10... | collective-permute-start | bytes 405512 | tf_op jit(solution)/shard_map/ppermute | solution.py:32
  20.1 2.2 %collective-permute-done.13.g3 = s16[264,256]{1,0:T(8,128)(2,1)S(1)} collective-permute-done((s16[264,256]{1,0:T(8,128)(2,1)S(1)}, s16[264,256]{1,0:T(8,128)(2,1)S(1)}, u32[]{:S(2)}, u32[]{:S(2)}) %collective-permute-start.13) | collective-permute-done | bytes 135200 | tf_op jit(solution)/shard_map/ppermute | solution.py:32
  22.9 4.3 %collective-permute-done.10.g3 = s16[264,256]{1,0:T(8,128)(2,1)S(1)} collective-permute-done((s16[264,256]{1,0:T(8,128)(2,1)S(1)}, s16[264,256]{1,0:T(8,128)(2,1)S(1)}, u32[]{:S(2)}, u32[]{:S(2)}) %collective-permute-start.10) | collective-permute-done | bytes 135200 | tf_op jit(solution)/shard_map/ppermute | solution.py:32
  27.1 3.2 %collective-permute-start.7 = (s16[264,256]{1,0:T(8,128)(2,1)S(1)}, s16[264,256]{1,0:T(8,128)(2,1)S(1)}, u32[]{:S(2)}, u32[]{:S(2)}) collective-permute-start(s16[264,256]{1,0:T(8,128)(2,1)S(1)} %get-tuple-element.35), channel_id=1, source_target_pairs={{0,24},{8,16},{16,8},{24,0},{1,25},{9,17},{17,9},{25,1},{2,26},{10... | collective-permute-start | bytes 405512 | tf_op jit(solution)/shard_map/ppermute | solution.py:32
  31.6 3.9 %collective-permute-start.3 = (s16[264,256]{1,0:T(8,128)(2,1)S(1)}, s16[264,256]{1,0:T(8,128)(2,1)S(1)}, u32[]{:S(2)}, u32[]{:S(2)}) collective-permute-start(s16[264,256]{1,0:T(8,128)(2,1)S(1)} %get-tuple-element.31), channel_id=1, source_target_pairs={{0,16},{8,24},{16,0},{24,8},{1,17},{9,25},{17,1},{25,9},{2,18},{10... | collective-permute-start | bytes 405512 | tf_op jit(solution)/shard_map/ppermute | solution.py:32
  37.4 2.2 %collective-permute-done.15.z2 = s16[264,256]{1,0:T(8,128)(2,1)S(1)} collective-permute-done((s16[264,256]{1,0:T(8,128)(2,1)S(1)}, s16[264,256]{1,0:T(8,128)(2,1)S(1)}, u32[]{:S(2)}, u32[]{:S(2)}) %collective-permute-start.15) | collective-permute-done | bytes 135200 | tf_op jit(solution)/shard_map/ppermute | solution.py:32
  42.7 4.4 %collective-permute-done.16.z3 = s16[264,256]{1,0:T(8,128)(2,1)S(1)} collective-permute-done((s16[264,256]{1,0:T(8,128)(2,1)S(1)}, s16[264,256]{1,0:T(8,128)(2,1)S(1)}, u32[]{:S(2)}, u32[]{:S(2)}) %collective-permute-start.16) | collective-permute-done | bytes 135200 | tf_op jit(solution)/shard_map/ppermute | solution.py:32
  50.5 2.1 %collective-permute-start.19 = (f32[1,1024]{1,0:T(1,128)S(1)}, f32[1,1024]{1,0:T(1,128)S(1)}, u32[]{:S(2)}, u32[]{:S(2)}) collective-permute-start(f32[1,1024]{1,0:T(1,128)S(1)} %get-tuple-element.44.refs_0_), channel_id=1, source_target_pairs={{0,96},{32,64},{64,32},{96,0},{128,224},{160,192},{192,160},{224,1... | collective-permute-start | bytes 12296 | tf_op jit(solution)/shard_map/ppermute | solution.py:32
  54.2 6.0 %collective-permute-start.20 = (f32[4,1024]{1,0:T(4,128)S(1)}, f32[4,1024]{1,0:T(4,128)S(1)}, u32[]{:S(2)}, u32[]{:S(2)}) collective-permute-start(f32[4,1024]{1,0:T(4,128)S(1)} %bundle.4.near), channel_id=1, source_target_pairs={{0,128},{32,160},{64,192},{96,224},{128,0},{160,32},{192,64},{224,... | collective-permute-start | bytes 49160 | tf_op jit(solution)/shard_map/ppermute | solution.py:32
  61.4 2.6 %master_step.1 = (f32[256,256]{1,0:T(8,128)}, bf16[256,256]{1,0:T(8,128)(2,1)S(1)}) custom-call(f32[256,256]{1,0:T(8,128)S(1)} %copy-done.2, f32[256,256]{1,0:T(8,128)S(1)} %copy-done, f32[4,1024]{1,0:T(4,128)S(1)} %bundle.4.near, f32[4,1024]{1,0:T(4,128)S(1)} %collective-permute-done.20.far), custom_call_target="tpu_custom_call" | custom-call | tf_op jit(solution)/shard_map/master_step/pallas_call | solution.py:261
  64.0 2.9 %collective-permute-start.21 = (bf16[256,256]{1,0:T(8,128)(2,1)S(1)}, bf16[256,256]{1,0:T(8,128)(2,1)S(1)}, u32[]{:S(2)}, u32[]{:S(2)}) collective-permute-start(bf16[256,256]{1,0:T(8,128)(2,1)S(1)} %get-tuple-element.46.refs_0_), channel_id=1, source_target_pairs={{0,6},{2,4},{4,2},{6,0},{1,7},{3,5},{5,3},{7,1},{8,14},{10,12},{12... | collective-permute-start | bytes 393224 | tf_op jit(solution)/shard_map/ppermute | solution.py:32
  67.2 3.4 %collective-permute-start.33 = (bf16[256,256]{1,0:T(8,128)(2,1)S(1)}, bf16[256,256]{1,0:T(8,128)(2,1)S(1)}, u32[]{:S(2)}, u32[]{:S(2)}) collective-permute-start(bf16[256,256]{1,0:T(8,128)(2,1)S(1)} %get-tuple-element.46.refs_0_), channel_id=1, source_target_pairs={{0,8},{8,0},{16,24},{24,16},{1,9},{9,1},{17,25},{25,17},{2,10},{10... | collective-permute-start | bytes 393224 | tf_op jit(solution)/shard_map/ppermute | solution.py:32
  72.4 2.1 %collective-permute-done.26.refs_2_ = bf16[256,256]{1,0:T(8,128)(2,1)S(1)} collective-permute-done((bf16[256,256]{1,0:T(8,128)(2,1)S(1)}, bf16[256,256]{1,0:T(8,128)(2,1)S(1)}, u32[]{:S(2)}, u32[]{:S(2)}) %collective-permute-start.26) | collective-permute-done | bytes 131104 | tf_op jit(solution)/shard_map/ppermute | solution.py:32
  74.5 6.0 %collective-permute-start.37 = (bf16[256,256]{1,0:T(8,128)(2,1)S(1)}, bf16[256,256]{1,0:T(8,128)(2,1)S(1)}, u32[]{:S(2)}, u32[]{:S(2)}) collective-permute-start(bf16[256,256]{1,0:T(8,128)(2,1)S(1)} %collective-permute-done.31.refs_1_), channel_id=1, source_target_pairs={{0,24},{8,16},{16,8},{24,0},{1,25},{9,17},{17,9},{25,1},{2,26},{10... | collective-permute-start | bytes 393224 | tf_op jit(solution)/shard_map/ppermute | solution.py:32
  80.6 4.2 %collective-permute-done.37.refs_9_ = bf16[256,256]{1,0:T(8,128)(2,1)S(1)} collective-permute-done((bf16[256,256]{1,0:T(8,128)(2,1)S(1)}, bf16[256,256]{1,0:T(8,128)(2,1)S(1)}, u32[]{:S(2)}, u32[]{:S(2)}) %collective-permute-start.37) | collective-permute-done | bytes 131104 | tf_op jit(solution)/shard_map/ppermute | solution.py:32
  86.6 2.9 %collective-permute-start.27 = (bf16[256,256]{1,0:T(8,128)(2,1)S(1)}, bf16[256,256]{1,0:T(8,128)(2,1)S(1)}, u32[]{:S(2)}, u32[]{:S(2)}) collective-permute-start(bf16[256,256]{1,0:T(8,128)(2,1)S(1)} %collective-permute-done.26.refs_2_), channel_id=1, source_target_pairs={{0,16},{8,24},{16,0},{24,8},{1,17},{9,25},{17,1},{25,9},{2,18},{10... | collective-permute-start | bytes 393224 | tf_op jit(solution)/shard_map/ppermute | solution.py:32
  89.8 2.9 %collective-permute-start.22 = (bf16[256,256]{1,0:T(8,128)(2,1)S(1)}, bf16[256,256]{1,0:T(8,128)(2,1)S(1)}, u32[]{:S(2)}, u32[]{:S(2)}) collective-permute-start(bf16[256,256]{1,0:T(8,128)(2,1)S(1)} %collective-permute-done.21.refs_3_), channel_id=1, source_target_pairs={{0,16},{8,24},{16,0},{24,8},{1,17},{9,25},{17,1},{25,9},{2,18},{10... | collective-permute-start | bytes 393224 | tf_op jit(solution)/shard_map/ppermute | solution.py:32
  93.9 2.3 %collective-permute-done.28.refs_1_ = bf16[256,256]{1,0:T(8,128)(2,1)S(1)} collective-permute-done((bf16[256,256]{1,0:T(8,128)(2,1)S(1)}, bf16[256,256]{1,0:T(8,128)(2,1)S(1)}, u32[]{:S(2)}, u32[]{:S(2)}) %collective-permute-start.28) | collective-permute-done | bytes 131104 | tf_op jit(solution)/shard_map/ppermute | solution.py:32
  96.3 3.5 %collective-permute-start.30 = (bf16[3,256,256]{2,1,0:T(8,128)(2,1)S(1)}, bf16[3,256,256]{2,1,0:T(8,128)(2,1)S(1)}, u32[]{:S(2)}, u32[]{:S(2)}) collective-permute-start(bf16[3,256,256]{2,1,0:T(8,128)(2,1)S(1)} %bundle.6.refs_0_), channel_id=1, source_target_pairs={{0,1},{1,0},{2,3},{3,2},{4,5},{5,4},{6,7},{7,6},{8,9},{9,8},{10,11... | collective-permute-start | bytes 1179656 | tf_op jit(solution)/shard_map/ppermute | solution.py:32
  101.8 2.2 %collective-permute-start.25 = (bf16[3,256,256]{2,1,0:T(8,128)(2,1)S(1)}, bf16[3,256,256]{2,1,0:T(8,128)(2,1)S(1)}, u32[]{:S(2)}, u32[]{:S(2)}) collective-permute-start(bf16[3,256,256]{2,1,0:T(8,128)(2,1)S(1)} %bundle.5.refs_0_), channel_id=1, source_target_pairs={{0,1},{1,0},{2,3},{3,2},{4,5},{5,4},{6,7},{7,6},{8,9},{9,8},{10,11... | collective-permute-start | bytes 1179656 | tf_op jit(solution)/shard_map/ppermute | solution.py:32
  104.0 2.0 %momentum_step.1 = f32[256,256]{1,0:T(8,128)} custom-call(f32[256,256]{1,0:T(8,128)S(1)} %get-tuple-element.42.acc, f32[256,256]{1,0:T(8,128)S(1)} %get-tuple-element.43.coeffs, f32[256,256]{1,0:T(8,128)S(1)} %copy-done, s32[1,512]{1,0:T(1,128)S(1)} %reshape_squeeze.3.ids), custom_call_target="tpu_custom_call" | custom-call | flops 1000000000 | bytes 1000000 | tf_op jit(solution)/shard_map/momentum_step/pallas_call | solution.py:199
  (80 shorter events, 30.8 us)
Async XLA Ops:
  4.2 11.3 %collective-permute-start = (bf16[256,3072]{1,0:T(8,128)(2,1)S(1)}, bf16[256,3072]{1,0:T(8,128)(2,1)S(1)}, u32[]{:S(2)}, u32[]{:S(2)}) collective-permute-start(bf16[256,3072]{1,0:T(8,128)(2,1)S(1)} %get-tuple-element.26), channel_id=1, source_target_pairs={{0,1},{1,0},{2,3},{3,2},{4,5},{5,4},{6,7},{7,6},{8,9},{9,8},{10,11... | collective-permute-start | bytes 4718600 | tf_op jit(solution)/shard_map/ppermute | solution.py:32
  11.6 8.5 %collective-permute-start.12 = (s16[264,256]{1,0:T(8,128)(2,1)S(1)}, s16[264,256]{1,0:T(8,128)(2,1)S(1)}, u32[]{:S(2)}, u32[]{:S(2)}) collective-permute-start(s16[264,256]{1,0:T(8,128)(2,1)S(1)} %get-tuple-element.40), channel_id=1, source_target_pairs={{0,16},{8,24},{16,0},{24,8},{1,17},{9,25},{17,1},{25,9},{2,18},{10... | collective-permute-start | bytes 405512 | tf_op jit(solution)/shard_map/ppermute | solution.py:32
  13.5 8.8 %collective-permute-start.13 = (s16[264,256]{1,0:T(8,128)(2,1)S(1)}, s16[264,256]{1,0:T(8,128)(2,1)S(1)}, u32[]{:S(2)}, u32[]{:S(2)}) collective-permute-start(s16[264,256]{1,0:T(8,128)(2,1)S(1)} %get-tuple-element.41), channel_id=1, source_target_pairs={{0,24},{8,16},{16,8},{24,0},{1,25},{9,17},{17,9},{25,1},{2,26},{10... | collective-permute-start | bytes 405512 | tf_op jit(solution)/shard_map/ppermute | solution.py:32
  16.2 11.0 %collective-permute-start.10 = (s16[264,256]{1,0:T(8,128)(2,1)S(1)}, s16[264,256]{1,0:T(8,128)(2,1)S(1)}, u32[]{:S(2)}, u32[]{:S(2)}) collective-permute-start(s16[264,256]{1,0:T(8,128)(2,1)S(1)} %get-tuple-element.38), channel_id=1, source_target_pairs={{0,24},{8,16},{16,8},{24,0},{1,25},{9,17},{17,9},{25,1},{2,26},{10... | collective-permute-start | bytes 405512 | tf_op jit(solution)/shard_map/ppermute | solution.py:32
  17.0 13.6 %collective-permute-start.8 = (s16[264,256]{1,0:T(8,128)(2,1)S(1)}, s16[264,256]{1,0:T(8,128)(2,1)S(1)}, u32[]{:S(2)}, u32[]{:S(2)}) collective-permute-start(s16[264,256]{1,0:T(8,128)(2,1)S(1)} %get-tuple-element.36), channel_id=1, source_target_pairs={{0,8},{8,0},{16,24},{24,16},{1,9},{9,1},{17,25},{25,17},{2,10},{10... | collective-permute-start | bytes 405512 | tf_op jit(solution)/shard_map/ppermute | solution.py:32
  17.0 14.4 %collective-permute-start.9 = (s16[264,256]{1,0:T(8,128)(2,1)S(1)}, s16[264,256]{1,0:T(8,128)(2,1)S(1)}, u32[]{:S(2)}, u32[]{:S(2)}) collective-permute-start(s16[264,256]{1,0:T(8,128)(2,1)S(1)} %get-tuple-element.37), channel_id=1, source_target_pairs={{0,16},{8,24},{16,0},{24,8},{1,17},{9,25},{17,1},{25,9},{2,18},{10... | collective-permute-start | bytes 405512 | tf_op jit(solution)/shard_map/ppermute | solution.py:32
  20.1 11.5 %collective-permute-start.5 = (s16[264,256]{1,0:T(8,128)(2,1)S(1)}, s16[264,256]{1,0:T(8,128)(2,1)S(1)}, u32[]{:S(2)}, u32[]{:S(2)}) collective-permute-start(s16[264,256]{1,0:T(8,128)(2,1)S(1)} %get-tuple-element.33), channel_id=1, source_target_pairs={{0,8},{8,0},{16,24},{24,16},{1,9},{9,1},{17,25},{25,17},{2,10},{10... | collective-permute-start | bytes 405512 | tf_op jit(solution)/shard_map/ppermute | solution.py:32
  22.3 13.2 %collective-permute-start.6 = (s16[264,256]{1,0:T(8,128)(2,1)S(1)}, s16[264,256]{1,0:T(8,128)(2,1)S(1)}, u32[]{:S(2)}, u32[]{:S(2)}) collective-permute-start(s16[264,256]{1,0:T(8,128)(2,1)S(1)} %get-tuple-element.34), channel_id=1, source_target_pairs={{0,16},{8,24},{16,0},{24,8},{1,17},{9,25},{17,1},{25,9},{2,18},{10... | collective-permute-start | bytes 405512 | tf_op jit(solution)/shard_map/ppermute | solution.py:32
  27.1 8.4 %collective-permute-start.7 = (s16[264,256]{1,0:T(8,128)(2,1)S(1)}, s16[264,256]{1,0:T(8,128)(2,1)S(1)}, u32[]{:S(2)}, u32[]{:S(2)}) collective-permute-start(s16[264,256]{1,0:T(8,128)(2,1)S(1)} %get-tuple-element.35), channel_id=1, source_target_pairs={{0,24},{8,16},{16,8},{24,0},{1,25},{9,17},{17,9},{25,1},{2,26},{10... | collective-permute-start | bytes 405512 | tf_op jit(solution)/shard_map/ppermute | solution.py:32
  30.6 9.1 %collective-permute-start.15 = (s16[264,256]{1,0:T(8,128)(2,1)S(1)}, s16[264,256]{1,0:T(8,128)(2,1)S(1)}, u32[]{:S(2)}, u32[]{:S(2)}) collective-permute-start(s16[264,256]{1,0:T(8,128)(2,1)S(1)} %octet_sums.3.refs_0_), channel_id=1, source_target_pairs={{0,4},{2,6},{4,0},{6,2},{1,5},{3,7},{5,1},{7,3},{8,12},{10,14},{12... | collective-permute-start | bytes 405512 | tf_op jit(solution)/shard_map/ppermute | solution.py:32
  31.4 10.0 %collective-permute-start.2 = (s16[264,256]{1,0:T(8,128)(2,1)S(1)}, s16[264,256]{1,0:T(8,128)(2,1)S(1)}, u32[]{:S(2)}, u32[]{:S(2)}) collective-permute-start(s16[264,256]{1,0:T(8,128)(2,1)S(1)} %get-tuple-element.30), channel_id=1, source_target_pairs={{0,8},{8,0},{16,24},{24,16},{1,9},{9,1},{17,25},{25,17},{2,10},{10... | collective-permute-start | bytes 405512 | tf_op jit(solution)/shard_map/ppermute | solution.py:32
  31.6 9.8 %collective-permute-start.3 = (s16[264,256]{1,0:T(8,128)(2,1)S(1)}, s16[264,256]{1,0:T(8,128)(2,1)S(1)}, u32[]{:S(2)}, u32[]{:S(2)}) collective-permute-start(s16[264,256]{1,0:T(8,128)(2,1)S(1)} %get-tuple-element.31), channel_id=1, source_target_pairs={{0,16},{8,24},{16,0},{24,8},{1,17},{9,25},{17,1},{25,9},{2,18},{10... | collective-permute-start | bytes 405512 | tf_op jit(solution)/shard_map/ppermute | solution.py:32
  35.5 7.2 %collective-permute-start.4 = (s16[264,256]{1,0:T(8,128)(2,1)S(1)}, s16[264,256]{1,0:T(8,128)(2,1)S(1)}, u32[]{:S(2)}, u32[]{:S(2)}) collective-permute-start(s16[264,256]{1,0:T(8,128)(2,1)S(1)} %get-tuple-element.32), channel_id=1, source_target_pairs={{0,24},{8,16},{16,8},{24,0},{1,25},{9,17},{17,9},{25,1},{2,26},{10... | collective-permute-start | bytes 405512 | tf_op jit(solution)/shard_map/ppermute | solution.py:32
  39.7 7.4 %collective-permute-start.16 = (s16[264,256]{1,0:T(8,128)(2,1)S(1)}, s16[264,256]{1,0:T(8,128)(2,1)S(1)}, u32[]{:S(2)}, u32[]{:S(2)}) collective-permute-start(s16[264,256]{1,0:T(8,128)(2,1)S(1)} %octet_sums.4.refs_0_), channel_id=1, source_target_pairs={{0,6},{2,4},{4,2},{6,0},{1,7},{3,5},{5,3},{7,1},{8,14},{10,12},{12... | collective-permute-start | bytes 405512 | tf_op jit(solution)/shard_map/ppermute | solution.py:32
  66.9 7.6 %collective-permute-start.26 = (bf16[256,256]{1,0:T(8,128)(2,1)S(1)}, bf16[256,256]{1,0:T(8,128)(2,1)S(1)}, u32[]{:S(2)}, u32[]{:S(2)}) collective-permute-start(bf16[256,256]{1,0:T(8,128)(2,1)S(1)} %get-tuple-element.46.refs_0_), channel_id=1, source_target_pairs={{0,4},{2,6},{4,0},{6,2},{1,5},{3,7},{5,1},{7,3},{8,12},{10,14},{12... | collective-permute-start | bytes 393224 | tf_op jit(solution)/shard_map/ppermute | solution.py:32
  67.2 7.3 %collective-permute-start.32 = (bf16[256,256]{1,0:T(8,128)(2,1)S(1)}, bf16[256,256]{1,0:T(8,128)(2,1)S(1)}, u32[]{:S(2)}, u32[]{:S(2)}) collective-permute-start(bf16[256,256]{1,0:T(8,128)(2,1)S(1)} %get-tuple-element.46.refs_0_), channel_id=1, source_target_pairs={{0,16},{8,24},{16,0},{24,8},{1,17},{9,25},{17,1},{25,9},{2,18},{10... | collective-permute-start | bytes 393224 | tf_op jit(solution)/shard_map/ppermute | solution.py:32
  67.2 13.4 %collective-permute-start.33 = (bf16[256,256]{1,0:T(8,128)(2,1)S(1)}, bf16[256,256]{1,0:T(8,128)(2,1)S(1)}, u32[]{:S(2)}, u32[]{:S(2)}) collective-permute-start(bf16[256,256]{1,0:T(8,128)(2,1)S(1)} %get-tuple-element.46.refs_0_), channel_id=1, source_target_pairs={{0,8},{8,0},{16,24},{24,16},{1,9},{9,1},{17,25},{25,17},{2,10},{10... | collective-permute-start | bytes 393224 | tf_op jit(solution)/shard_map/ppermute | solution.py:32
  70.6 10.0 %collective-permute-start.34 = (bf16[256,256]{1,0:T(8,128)(2,1)S(1)}, bf16[256,256]{1,0:T(8,128)(2,1)S(1)}, u32[]{:S(2)}, u32[]{:S(2)}) collective-permute-start(bf16[256,256]{1,0:T(8,128)(2,1)S(1)} %get-tuple-element.46.refs_0_), channel_id=1, source_target_pairs={{0,24},{8,16},{16,8},{24,0},{1,25},{9,17},{17,9},{25,1},{2,26},{10... | collective-permute-start | bytes 393224 | tf_op jit(solution)/shard_map/ppermute | solution.py:32
  70.9 9.7 %collective-permute-start.35 = (bf16[256,256]{1,0:T(8,128)(2,1)S(1)}, bf16[256,256]{1,0:T(8,128)(2,1)S(1)}, u32[]{:S(2)}, u32[]{:S(2)}) collective-permute-start(bf16[256,256]{1,0:T(8,128)(2,1)S(1)} %collective-permute-done.31.refs_1_), channel_id=1, source_target_pairs={{0,16},{8,24},{16,0},{24,8},{1,17},{9,25},{17,1},{25,9},{2,18},{10... | collective-permute-start | bytes 393224 | tf_op jit(solution)/shard_map/ppermute | solution.py:32
  74.5 10.2 %collective-permute-start.37 = (bf16[256,256]{1,0:T(8,128)(2,1)S(1)}, bf16[256,256]{1,0:T(8,128)(2,1)S(1)}, u32[]{:S(2)}, u32[]{:S(2)}) collective-permute-start(bf16[256,256]{1,0:T(8,128)(2,1)S(1)} %collective-permute-done.31.refs_1_), channel_id=1, source_target_pairs={{0,24},{8,16},{16,8},{24,0},{1,25},{9,17},{17,9},{25,1},{2,26},{10... | collective-permute-start | bytes 393224 | tf_op jit(solution)/shard_map/ppermute | solution.py:32
  84.8 21.1 %collective-permute-start.38 = (bf16[10,256,256]{2,1,0:T(8,128)(2,1)S(1)}, bf16[10,256,256]{2,1,0:T(8,128)(2,1)S(1)}, u32[]{:S(2)}, u32[]{:S(2)}) collective-permute-start(bf16[10,256,256]{2,1,0:T(8,128)(2,1)S(1)} %bundle.7.refs_0_), channel_id=1, source_target_pairs={{0,1},{1,0},{2,3},{3,2},{4,5},{5,4},{6,7},{7,6},{8,9},{9,8},{10,11... | collective-permute-start | bytes 3932168 | tf_op jit(solution)/shard_map/ppermute | solution.py:32
  89.8 10.0 %collective-permute-start.22 = (bf16[256,256]{1,0:T(8,128)(2,1)S(1)}, bf16[256,256]{1,0:T(8,128)(2,1)S(1)}, u32[]{:S(2)}, u32[]{:S(2)}) collective-permute-start(bf16[256,256]{1,0:T(8,128)(2,1)S(1)} %collective-permute-done.21.refs_3_), channel_id=1, source_target_pairs={{0,16},{8,24},{16,0},{24,8},{1,17},{9,25},{17,1},{25,9},{2,18},{10... | collective-permute-start | bytes 393224 | tf_op jit(solution)/shard_map/ppermute | solution.py:32
  93.0 8.7 %collective-permute-start.23 = (bf16[256,256]{1,0:T(8,128)(2,1)S(1)}, bf16[256,256]{1,0:T(8,128)(2,1)S(1)}, u32[]{:S(2)}, u32[]{:S(2)}) collective-permute-start(bf16[256,256]{1,0:T(8,128)(2,1)S(1)} %collective-permute-done.21.refs_3_), channel_id=1, source_target_pairs={{0,8},{8,0},{16,24},{24,16},{1,9},{9,1},{17,25},{25,17},{2,10},{10... | collective-permute-start | bytes 393224 | tf_op jit(solution)/shard_map/ppermute | solution.py:32
  96.3 11.3 %collective-permute-start.30 = (bf16[3,256,256]{2,1,0:T(8,128)(2,1)S(1)}, bf16[3,256,256]{2,1,0:T(8,128)(2,1)S(1)}, u32[]{:S(2)}, u32[]{:S(2)}) collective-permute-start(bf16[3,256,256]{2,1,0:T(8,128)(2,1)S(1)} %bundle.6.refs_0_), channel_id=1, source_target_pairs={{0,1},{1,0},{2,3},{3,2},{4,5},{5,4},{6,7},{7,6},{8,9},{9,8},{10,11... | collective-permute-start | bytes 1179656 | tf_op jit(solution)/shard_map/ppermute | solution.py:32
  (19 other events, 156.3 us)

commit v2 on v1

--- a/solution.py
+++ b/solution.py
@@ -229,29 +229,46 @@
     )(*parts)
 
 
+def union_of(notes, me):
+    rows = [notes[r : r + 1, :] for r in range(4)]
+    ordered = []
+    for q in range(4):
+        rel = (me & 3) ^ q
+        found = rows[0]
+        for r in range(1, 4):
+            found = jnp.where(rel == r, rows[r], found)
+        ordered.append(found)
+    bands = []
+    for a in range(4):
+        v = jnp.concatenate([x[:, a * 128 : a * 128 + 128] for x in ordered], axis=1)
+        k = jnp.concatenate([x[:, 512 + a * 128 : 640 + a * 128] for x in ordered], axis=1).astype(jnp.int32)
+        lane = lax.broadcasted_iota(jnp.int32, (1, 512), 1)
+        row = lax.broadcasted_iota(jnp.int32, (BLOCK, 512), 0) == (k >> 6)
+        col = lax.broadcasted_iota(jnp.int32, (W, 512), 0) == (((lane >> 5) & 3) * BLOCK + (k & 63))
+        col = col.astype(jnp.float32).astype(jnp.bfloat16)
+        stack = jnp.concatenate([jnp.where(row, p.astype(jnp.float32), 0.0).astype(jnp.bfloat16) for p in thirds(v)], axis=0)
+        both = dot(stack, col, ((1,), (1,)))
+        bands.append(both[0:BLOCK] + (both[BLOCK : 2 * BLOCK] + both[2 * BLOCK :]))
+    return jnp.concatenate(bands, axis=0)
+
+
+def near_union(notes):
+    def body(notes, out):
+        out[...] = union_of(notes, lax.axis_index("group"))
+
+    return pl.pallas_call(
+        body,
+        out_shape=jax.ShapeDtypeStruct((W, W), jnp.float32),
+        in_specs=[VM],
+        out_specs=VM,
+        compiler_params=params(16),
+        name="near_union",
+    )(notes)
+
+
 def master_step(master, table, near, far):
     def body(master, table, near, far, out, low):
-        me = lax.axis_index("group")
-        notes = [near[i : i + 1, :] for i in range(4)] + [far[i : i + 1, :] for i in range(4)]
-        ordered = []
-        for g in range(8):
-            rel = me ^ g
-            found = notes[0]
-            for r in range(1, 8):
-                found = jnp.where(rel == r, notes[r], found)
-            ordered.append(found)
-        bands = []
-        for a in range(4):
-            v = jnp.concatenate([x[:, a * 128 : a * 128 + 128] for x in ordered], axis=1)
-            k = jnp.concatenate([x[:, 512 + a * 128 : 640 + a * 128] for x in ordered], axis=1).astype(jnp.int32)
-            lane = lax.broadcasted_iota(jnp.int32, (1, 1024), 1)
-            row = lax.broadcasted_iota(jnp.int32, (BLOCK, 1024), 0) == (k >> 6)
-            col = lax.broadcasted_iota(jnp.int32, (W, 1024), 0) == (((lane >> 5) & 3) * BLOCK + (k & 63))
-            col = col.astype(jnp.float32).astype(jnp.bfloat16)
-            stack = jnp.concatenate([jnp.where(row, p.astype(jnp.float32), 0.0).astype(jnp.bfloat16) for p in thirds(v)], axis=0)
-            both = dot(stack, col, ((1,), (1,)))
-            bands.append(both[0:BLOCK] + (both[BLOCK : 2 * BLOCK] + both[2 * BLOCK :]))
-        union = jnp.concatenate(bands, axis=0)
+        union = near[...] + union_of(far, lax.axis_index("group"))
         t = table[...]
         change = dot(dot(t, union, ((0,), (0,)), HI), t, precision=HI)
         result = master[...] - STEP * jnp.tanh(change)
@@ -322,7 +339,8 @@
     momentum_out = momentum_step(acc, coeffs, table, ids)
     mine = bundle(notes, flat=True)
     theirs = swapped(mine, "group", 4)
-    master_out, low = master_step(master, table, mine, theirs)
+    partly = near_union(mine)
+    master_out, low = master_step(master, table, partly, theirs)
 
     by_z = [low] + [swapped(low, "z", e) for e in (1, 2, 3)]
     by_x = {(d, e): swapped(by_z[e], "x", d) for e in range(4) for d in NEXT}

time: 110 us -> 109 us (level)
  no operation moved by 1% of the time
where the time goes in v2:
time: 109 us
  starting transfers between devices  62.2 us (57%)
  waiting for transfers between devices  31 us (28%)
  Pallas kernels  15 us (14%)
    ppermute x39, starting transfers between devices, swapped(): return lax.ppermute(value, axis, [(i, i ^ mask) for i in range(size)])  62.2 us
    ppermute x39, waiting for transfers between devices, swapped(): return lax.ppermute(value, axis, [(i, i ^ mask) for i in range(size)])  31 us
    pallas_call x2, Pallas kernels, pick_out(): pl.pallas_call(body, out_shape=tuple((jax.ShapeDtypeStruct((W, 4 * len(zs...  3.55 us
    pallas_call x3, Pallas kernels, joined(): pl.pallas_call(body, out_shape=jax.ShapeDtypeStruct((W, 32 * W), jnp.bflo...  3.53 us
    pallas_call x1, Pallas kernels, master_step(): pl.pallas_call(body, out_shape=(jax.ShapeDtypeStruct((W, W), jnp.float32)...  2.24 us
  transfers between devices with their start and end apart: 39, of which 14 were waited for; matrix products, arithmetic and copies ran while one was open for 0% of the time, Pallas kernels for 6%

profile of v2, /device:TPU:1, one launch (start us, length us, event | category | flops | bytes accessed | tf_op | source)
XLA Modules:
  0.0 109.3 jit_solution(2052389905707582329)
XLA Ops:
  1.8 2.4 %pick_out.3 = (bf16[256,1024]{1,0:T(8,128)(2,1)S(1)}, bf16[256,3072]{1,0:T(8,128)(2,1)S(1)}, bf16[256,3072]{1,0:T(8,128)(2,1)S(1)}) custom-call(bf16[256,8192]{1,0:T(8,128)(2,1)} %bitcast.5, bf16[256,1024]{1,0:T(8,128)(2,1)S(1)} %pick_out.2.refs_0_), custom_call_target="tpu_custom_call" | custom-call | tf_op jit(solution)/shard_map/pick_out/pallas_call | solution.py:79
  4.2 3.3 %collective-permute-start = (bf16[256,3072]{1,0:T(8,128)(2,1)S(1)}, bf16[256,3072]{1,0:T(8,128)(2,1)S(1)}, u32[]{:S(2)}, u32[]{:S(2)}) collective-permute-start(bf16[256,3072]{1,0:T(8,128)(2,1)S(1)} %get-tuple-element.26), channel_id=1, source_target_pairs={{0,1},{1,0},{2,3},{3,2},{4,5},{5,4},{6,7},{7,6},{8,9},{9,8},{10,11... | collective-permute-start | bytes 4718600 | tf_op jit(solution)/shard_map/ppermute | solution.py:32
  7.6 3.7 %collective-permute-done.1.o = bf16[256,1024]{1,0:T(8,128)(2,1)S(1)} collective-permute-done((bf16[256,1024]{1,0:T(8,128)(2,1)S(1)}, bf16[256,1024]{1,0:T(8,128)(2,1)S(1)}, u32[]{:S(2)}, u32[]{:S(2)}) %collective-permute-start.1) | collective-permute-done | bytes 524320 | tf_op jit(solution)/shard_map/ppermute | solution.py:32
  17.0 3.1 %collective-permute-start.9 = (s16[264,256]{1,0:T(8,128)(2,1)S(1)}, s16[264,256]{1,0:T(8,128)(2,1)S(1)}, u32[]{:S(2)}, u32[]{:S(2)}) collective-permute-start(s16[264,256]{1,0:T(8,128)(2,1)S(1)} %get-tuple-element.37), channel_id=1, source_target_pairs={{0,16},{8,24},{16,0},{24,8},{1,17},{9,25},{17,1},{25,9},{2,18},{10... | collective-permute-start | bytes 405512 | tf_op jit(solution)/shard_map/ppermute | solution.py:32
  20.1 2.2 %collective-permute-done.13.g3 = s16[264,256]{1,0:T(8,128)(2,1)S(1)} collective-permute-done((s16[264,256]{1,0:T(8,128)(2,1)S(1)}, s16[264,256]{1,0:T(8,128)(2,1)S(1)}, u32[]{:S(2)}, u32[]{:S(2)}) %collective-permute-start.13) | collective-permute-done | bytes 135200 | tf_op jit(solution)/shard_map/ppermute | solution.py:32
  22.9 4.3 %collective-permute-done.10.g3 = s16[264,256]{1,0:T(8,128)(2,1)S(1)} collective-permute-done((s16[264,256]{1,0:T(8,128)(2,1)S(1)}, s16[264,256]{1,0:T(8,128)(2,1)S(1)}, u32[]{:S(2)}, u32[]{:S(2)}) %collective-permute-start.10) | collective-permute-done | bytes 135200 | tf_op jit(solution)/shard_map/ppermute | solution.py:32
  27.1 3.2 %collective-permute-start.7 = (s16[264,256]{1,0:T(8,128)(2,1)S(1)}, s16[264,256]{1,0:T(8,128)(2,1)S(1)}, u32[]{:S(2)}, u32[]{:S(2)}) collective-permute-start(s16[264,256]{1,0:T(8,128)(2,1)S(1)} %get-tuple-element.35), channel_id=1, source_target_pairs={{0,24},{8,16},{16,8},{24,0},{1,25},{9,17},{17,9},{25,1},{2,26},{10... | collective-permute-start | bytes 405512 | tf_op jit(solution)/shard_map/ppermute | solution.py:32
  31.6 3.9 %collective-permute-start.3 = (s16[264,256]{1,0:T(8,128)(2,1)S(1)}, s16[264,256]{1,0:T(8,128)(2,1)S(1)}, u32[]{:S(2)}, u32[]{:S(2)}) collective-permute-start(s16[264,256]{1,0:T(8,128)(2,1)S(1)} %get-tuple-element.31), channel_id=1, source_target_pairs={{0,16},{8,24},{16,0},{24,8},{1,17},{9,25},{17,1},{25,9},{2,18},{10... | collective-permute-start | bytes 405512 | tf_op jit(solution)/shard_map/ppermute | solution.py:32
  37.4 2.2 %collective-permute-done.15.z2 = s16[264,256]{1,0:T(8,128)(2,1)S(1)} collective-permute-done((s16[264,256]{1,0:T(8,128)(2,1)S(1)}, s16[264,256]{1,0:T(8,128)(2,1)S(1)}, u32[]{:S(2)}, u32[]{:S(2)}) %collective-permute-start.15) | collective-permute-done | bytes 135200 | tf_op jit(solution)/shard_map/ppermute | solution.py:32
  42.7 4.4 %collective-permute-done.16.z3 = s16[264,256]{1,0:T(8,128)(2,1)S(1)} collective-permute-done((s16[264,256]{1,0:T(8,128)(2,1)S(1)}, s16[264,256]{1,0:T(8,128)(2,1)S(1)}, u32[]{:S(2)}, u32[]{:S(2)}) %collective-permute-start.16) | collective-permute-done | bytes 135200 | tf_op jit(solution)/shard_map/ppermute | solution.py:32
  50.4 2.2 %collective-permute-start.19 = (f32[1,1024]{1,0:T(1,128)S(1)}, f32[1,1024]{1,0:T(1,128)S(1)}, u32[]{:S(2)}, u32[]{:S(2)}) collective-permute-start(f32[1,1024]{1,0:T(1,128)S(1)} %get-tuple-element.44.refs_0_), channel_id=1, source_target_pairs={{0,96},{32,64},{64,32},{96,0},{128,224},{160,192},{192,160},{224,1... | collective-permute-start | bytes 12296 | tf_op jit(solution)/shard_map/ppermute | solution.py:32
  54.1 6.1 %collective-permute-start.20 = (f32[4,1024]{1,0:T(4,128)S(1)}, f32[4,1024]{1,0:T(4,128)S(1)}, u32[]{:S(2)}, u32[]{:S(2)}) collective-permute-start(f32[4,1024]{1,0:T(4,128)S(1)} %bundle.4.notes), channel_id=1, source_target_pairs={{0,128},{32,160},{64,192},{96,224},{128,0},{160,32},{192,64},{224,... | collective-permute-start | bytes 49160 | tf_op jit(solution)/shard_map/ppermute | solution.py:32
  61.4 2.2 %master_step.1 = (f32[256,256]{1,0:T(8,128)}, bf16[256,256]{1,0:T(8,128)(2,1)S(1)}) custom-call(f32[256,256]{1,0:T(8,128)S(1)} %copy-done.2, f32[256,256]{1,0:T(8,128)S(1)} %copy-done, f32[256,256]{1,0:T(8,128)S(1)} %near_union.1.near, f32[4,1024]{1,0:T(4,128)S(1)} %collective-permute-done.20.far), custom_call_target="tpu_custom_call" | custom-call | tf_op jit(solution)/shard_map/master_step/pallas_call | solution.py:278
  63.6 2.9 %collective-permute-start.21 = (bf16[256,256]{1,0:T(8,128)(2,1)S(1)}, bf16[256,256]{1,0:T(8,128)(2,1)S(1)}, u32[]{:S(2)}, u32[]{:S(2)}) collective-permute-start(bf16[256,256]{1,0:T(8,128)(2,1)S(1)} %get-tuple-element.46.refs_0_), channel_id=1, source_target_pairs={{0,6},{2,4},{4,2},{6,0},{1,7},{3,5},{5,3},{7,1},{8,14},{10,12},{12... | collective-permute-start | bytes 393224 | tf_op jit(solution)/shard_map/ppermute | solution.py:32
  66.8 3.4 %collective-permute-start.33 = (bf16[256,256]{1,0:T(8,128)(2,1)S(1)}, bf16[256,256]{1,0:T(8,128)(2,1)S(1)}, u32[]{:S(2)}, u32[]{:S(2)}) collective-permute-start(bf16[256,256]{1,0:T(8,128)(2,1)S(1)} %get-tuple-element.46.refs_0_), channel_id=1, source_target_pairs={{0,8},{8,0},{16,24},{24,16},{1,9},{9,1},{17,25},{25,17},{2,10},{10... | collective-permute-start | bytes 393224 | tf_op jit(solution)/shard_map/ppermute | solution.py:32
  72.0 2.2 %collective-permute-done.26.refs_2_ = bf16[256,256]{1,0:T(8,128)(2,1)S(1)} collective-permute-done((bf16[256,256]{1,0:T(8,128)(2,1)S(1)}, bf16[256,256]{1,0:T(8,128)(2,1)S(1)}, u32[]{:S(2)}, u32[]{:S(2)}) %collective-permute-start.26) | collective-permute-done | bytes 131104 | tf_op jit(solution)/shard_map/ppermute | solution.py:32
  74.1 6.0 %collective-permute-start.37 = (bf16[256,256]{1,0:T(8,128)(2,1)S(1)}, bf16[256,256]{1,0:T(8,128)(2,1)S(1)}, u32[]{:S(2)}, u32[]{:S(2)}) collective-permute-start(bf16[256,256]{1,0:T(8,128)(2,1)S(1)} %collective-permute-done.31.refs_1_), channel_id=1, source_target_pairs={{0,24},{8,16},{16,8},{24,0},{1,25},{9,17},{17,9},{25,1},{2,26},{10... | collective-permute-start | bytes 393224 | tf_op jit(solution)/shard_map/ppermute | solution.py:32
  80.1 4.1 %collective-permute-done.37.refs_9_ = bf16[256,256]{1,0:T(8,128)(2,1)S(1)} collective-permute-done((bf16[256,256]{1,0:T(8,128)(2,1)S(1)}, bf16[256,256]{1,0:T(8,128)(2,1)S(1)}, u32[]{:S(2)}, u32[]{:S(2)}) %collective-permute-start.37) | collective-permute-done | bytes 131104 | tf_op jit(solution)/shard_map/ppermute | solution.py:32
  86.2 2.9 %collective-permute-start.27 = (bf16[256,256]{1,0:T(8,128)(2,1)S(1)}, bf16[256,256]{1,0:T(8,128)(2,1)S(1)}, u32[]{:S(2)}, u32[]{:S(2)}) collective-permute-start(bf16[256,256]{1,0:T(8,128)(2,1)S(1)} %collective-permute-done.26.refs_2_), channel_id=1, source_target_pairs={{0,16},{8,24},{16,0},{24,8},{1,17},{9,25},{17,1},{25,9},{2,18},{10... | collective-permute-start | bytes 393224 | tf_op jit(solution)/shard_map/ppermute | solution.py:32
  89.4 2.9 %collective-permute-start.22 = (bf16[256,256]{1,0:T(8,128)(2,1)S(1)}, bf16[256,256]{1,0:T(8,128)(2,1)S(1)}, u32[]{:S(2)}, u32[]{:S(2)}) collective-permute-start(bf16[256,256]{1,0:T(8,128)(2,1)S(1)} %collective-permute-done.21.refs_3_), channel_id=1, source_target_pairs={{0,16},{8,24},{16,0},{24,8},{1,17},{9,25},{17,1},{25,9},{2,18},{10... | collective-permute-start | bytes 393224 | tf_op jit(solution)/shard_map/ppermute | solution.py:32
  93.5 2.3 %collective-permute-done.28.refs_1_ = bf16[256,256]{1,0:T(8,128)(2,1)S(1)} collective-permute-done((bf16[256,256]{1,0:T(8,128)(2,1)S(1)}, bf16[256,256]{1,0:T(8,128)(2,1)S(1)}, u32[]{:S(2)}, u32[]{:S(2)}) %collective-permute-start.28) | collective-permute-done | bytes 131104 | tf_op jit(solution)/shard_map/ppermute | solution.py:32
  95.9 3.5 %collective-permute-start.30 = (bf16[3,256,256]{2,1,0:T(8,128)(2,1)S(1)}, bf16[3,256,256]{2,1,0:T(8,128)(2,1)S(1)}, u32[]{:S(2)}, u32[]{:S(2)}) collective-permute-start(bf16[3,256,256]{2,1,0:T(8,128)(2,1)S(1)} %bundle.6.refs_0_), channel_id=1, source_target_pairs={{0,1},{1,0},{2,3},{3,2},{4,5},{5,4},{6,7},{7,6},{8,9},{9,8},{10,11... | collective-permute-start | bytes 1179656 | tf_op jit(solution)/shard_map/ppermute | solution.py:32
  101.4 2.2 %collective-permute-start.25 = (bf16[3,256,256]{2,1,0:T(8,128)(2,1)S(1)}, bf16[3,256,256]{2,1,0:T(8,128)(2,1)S(1)}, u32[]{:S(2)}, u32[]{:S(2)}) collective-permute-start(bf16[3,256,256]{2,1,0:T(8,128)(2,1)S(1)} %bundle.5.refs_0_), channel_id=1, source_target_pairs={{0,1},{1,0},{2,3},{3,2},{4,5},{5,4},{6,7},{7,6},{8,9},{9,8},{10,11... | collective-permute-start | bytes 1179656 | tf_op jit(solution)/shard_map/ppermute | solution.py:32
  103.6 2.0 %momentum_step.1 = f32[256,256]{1,0:T(8,128)} custom-call(f32[256,256]{1,0:T(8,128)S(1)} %get-tuple-element.42.acc, f32[256,256]{1,0:T(8,128)S(1)} %get-tuple-element.43.coeffs, f32[256,256]{1,0:T(8,128)S(1)} %copy-done, s32[1,512]{1,0:T(1,128)S(1)} %reshape_squeeze.3.ids), custom_call_target="tpu_custom_call" | custom-call | flops 1000000000 | bytes 1000000 | tf_op jit(solution)/shard_map/momentum_step/pallas_call | solution.py:199
  (81 shorter events, 30.7 us)
Async XLA Ops:
  4.2 11.3 %collective-permute-start = (bf16[256,3072]{1,0:T(8,128)(2,1)S(1)}, bf16[256,3072]{1,0:T(8,128)(2,1)S(1)}, u32[]{:S(2)}, u32[]{:S(2)}) collective-permute-start(bf16[256,3072]{1,0:T(8,128)(2,1)S(1)} %get-tuple-element.26), channel_id=1, source_target_pairs={{0,1},{1,0},{2,3},{3,2},{4,5},{5,4},{6,7},{7,6},{8,9},{9,8},{10,11... | collective-permute-start | bytes 4718600 | tf_op jit(solution)/shard_map/ppermute | solution.py:32
  11.6 8.5 %collective-permute-start.12 = (s16[264,256]{1,0:T(8,128)(2,1)S(1)}, s16[264,256]{1,0:T(8,128)(2,1)S(1)}, u32[]{:S(2)}, u32[]{:S(2)}) collective-permute-start(s16[264,256]{1,0:T(8,128)(2,1)S(1)} %get-tuple-element.40), channel_id=1, source_target_pairs={{0,16},{8,24},{16,0},{24,8},{1,17},{9,25},{17,1},{25,9},{2,18},{10... | collective-permute-start | bytes 405512 | tf_op jit(solution)/shard_map/ppermute | solution.py:32
  13.5 8.8 %collective-permute-start.13 = (s16[264,256]{1,0:T(8,128)(2,1)S(1)}, s16[264,256]{1,0:T(8,128)(2,1)S(1)}, u32[]{:S(2)}, u32[]{:S(2)}) collective-permute-start(s16[264,256]{1,0:T(8,128)(2,1)S(1)} %get-tuple-element.41), channel_id=1, source_target_pairs={{0,24},{8,16},{16,8},{24,0},{1,25},{9,17},{17,9},{25,1},{2,26},{10... | collective-permute-start | bytes 405512 | tf_op jit(solution)/shard_map/ppermute | solution.py:32
  16.2 11.0 %collective-permute-start.10 = (s16[264,256]{1,0:T(8,128)(2,1)S(1)}, s16[264,256]{1,0:T(8,128)(2,1)S(1)}, u32[]{:S(2)}, u32[]{:S(2)}) collective-permute-start(s16[264,256]{1,0:T(8,128)(2,1)S(1)} %get-tuple-element.38), channel_id=1, source_target_pairs={{0,24},{8,16},{16,8},{24,0},{1,25},{9,17},{17,9},{25,1},{2,26},{10... | collective-permute-start | bytes 405512 | tf_op jit(solution)/shard_map/ppermute | solution.py:32
  17.0 13.6 %collective-permute-start.8 = (s16[264,256]{1,0:T(8,128)(2,1)S(1)}, s16[264,256]{1,0:T(8,128)(2,1)S(1)}, u32[]{:S(2)}, u32[]{:S(2)}) collective-permute-start(s16[264,256]{1,0:T(8,128)(2,1)S(1)} %get-tuple-element.36), channel_id=1, source_target_pairs={{0,8},{8,0},{16,24},{24,16},{1,9},{9,1},{17,25},{25,17},{2,10},{10... | collective-permute-start | bytes 405512 | tf_op jit(solution)/shard_map/ppermute | solution.py:32
  17.0 14.4 %collective-permute-start.9 = (s16[264,256]{1,0:T(8,128)(2,1)S(1)}, s16[264,256]{1,0:T(8,128)(2,1)S(1)}, u32[]{:S(2)}, u32[]{:S(2)}) collective-permute-start(s16[264,256]{1,0:T(8,128)(2,1)S(1)} %get-tuple-element.37), channel_id=1, source_target_pairs={{0,16},{8,24},{16,0},{24,8},{1,17},{9,25},{17,1},{25,9},{2,18},{10... | collective-permute-start | bytes 405512 | tf_op jit(solution)/shard_map/ppermute | solution.py:32
  20.1 11.5 %collective-permute-start.5 = (s16[264,256]{1,0:T(8,128)(2,1)S(1)}, s16[264,256]{1,0:T(8,128)(2,1)S(1)}, u32[]{:S(2)}, u32[]{:S(2)}) collective-permute-start(s16[264,256]{1,0:T(8,128)(2,1)S(1)} %get-tuple-element.33), channel_id=1, source_target_pairs={{0,8},{8,0},{16,24},{24,16},{1,9},{9,1},{17,25},{25,17},{2,10},{10... | collective-permute-start | bytes 405512 | tf_op jit(solution)/shard_map/ppermute | solution.py:32
  22.3 13.2 %collective-permute-start.6 = (s16[264,256]{1,0:T(8,128)(2,1)S(1)}, s16[264,256]{1,0:T(8,128)(2,1)S(1)}, u32[]{:S(2)}, u32[]{:S(2)}) collective-permute-start(s16[264,256]{1,0:T(8,128)(2,1)S(1)} %get-tuple-element.34), channel_id=1, source_target_pairs={{0,16},{8,24},{16,0},{24,8},{1,17},{9,25},{17,1},{25,9},{2,18},{10... | collective-permute-start | bytes 405512 | tf_op jit(solution)/shard_map/ppermute | solution.py:32
  27.1 8.4 %collective-permute-start.7 = (s16[264,256]{1,0:T(8,128)(2,1)S(1)}, s16[264,256]{1,0:T(8,128)(2,1)S(1)}, u32[]{:S(2)}, u32[]{:S(2)}) collective-permute-start(s16[264,256]{1,0:T(8,128)(2,1)S(1)} %get-tuple-element.35), channel_id=1, source_target_pairs={{0,24},{8,16},{16,8},{24,0},{1,25},{9,17},{17,9},{25,1},{2,26},{10... | collective-permute-start | bytes 405512 | tf_op jit(solution)/shard_map/ppermute | solution.py:32
  30.6 9.1 %collective-permute-start.15 = (s16[264,256]{1,0:T(8,128)(2,1)S(1)}, s16[264,256]{1,0:T(8,128)(2,1)S(1)}, u32[]{:S(2)}, u32[]{:S(2)}) collective-permute-start(s16[264,256]{1,0:T(8,128)(2,1)S(1)} %octet_sums.3.refs_0_), channel_id=1, source_target_pairs={{0,4},{2,6},{4,0},{6,2},{1,5},{3,7},{5,1},{7,3},{8,12},{10,14},{12... | collective-permute-start | bytes 405512 | tf_op jit(solution)/shard_map/ppermute | solution.py:32
  31.4 10.0 %collective-permute-start.2 = (s16[264,256]{1,0:T(8,128)(2,1)S(1)}, s16[264,256]{1,0:T(8,128)(2,1)S(1)}, u32[]{:S(2)}, u32[]{:S(2)}) collective-permute-start(s16[264,256]{1,0:T(8,128)(2,1)S(1)} %get-tuple-element.30), channel_id=1, source_target_pairs={{0,8},{8,0},{16,24},{24,16},{1,9},{9,1},{17,25},{25,17},{2,10},{10... | collective-permute-start | bytes 405512 | tf_op jit(solution)/shard_map/ppermute | solution.py:32
  31.6 9.8 %collective-permute-start.3 = (s16[264,256]{1,0:T(8,128)(2,1)S(1)}, s16[264,256]{1,0:T(8,128)(2,1)S(1)}, u32[]{:S(2)}, u32[]{:S(2)}) collective-permute-start(s16[264,256]{1,0:T(8,128)(2,1)S(1)} %get-tuple-element.31), channel_id=1, source_target_pairs={{0,16},{8,24},{16,0},{24,8},{1,17},{9,25},{17,1},{25,9},{2,18},{10... | collective-permute-start | bytes 405512 | tf_op jit(solution)/shard_map/ppermute | solution.py:32
  39.7 7.4 %collective-permute-start.16 = (s16[264,256]{1,0:T(8,128)(2,1)S(1)}, s16[264,256]{1,0:T(8,128)(2,1)S(1)}, u32[]{:S(2)}, u32[]{:S(2)}) collective-permute-start(s16[264,256]{1,0:T(8,128)(2,1)S(1)} %octet_sums.4.refs_0_), channel_id=1, source_target_pairs={{0,6},{2,4},{4,2},{6,0},{1,7},{3,5},{5,3},{7,1},{8,14},{10,12},{12... | collective-permute-start | bytes 405512 | tf_op jit(solution)/shard_map/ppermute | solution.py:32
  54.1 7.3 %collective-permute-start.20 = (f32[4,1024]{1,0:T(4,128)S(1)}, f32[4,1024]{1,0:T(4,128)S(1)}, u32[]{:S(2)}, u32[]{:S(2)}) collective-permute-start(f32[4,1024]{1,0:T(4,128)S(1)} %bundle.4.notes), channel_id=1, source_target_pairs={{0,128},{32,160},{64,192},{96,224},{128,0},{160,32},{192,64},{224,... | collective-permute-start | bytes 49160 | tf_op jit(solution)/shard_map/ppermute | solution.py:32
  66.5 7.6 %collective-permute-start.26 = (bf16[256,256]{1,0:T(8,128)(2,1)S(1)}, bf16[256,256]{1,0:T(8,128)(2,1)S(1)}, u32[]{:S(2)}, u32[]{:S(2)}) collective-permute-start(bf16[256,256]{1,0:T(8,128)(2,1)S(1)} %get-tuple-element.46.refs_0_), channel_id=1, source_target_pairs={{0,4},{2,6},{4,0},{6,2},{1,5},{3,7},{5,1},{7,3},{8,12},{10,14},{12... | collective-permute-start | bytes 393224 | tf_op jit(solution)/shard_map/ppermute | solution.py:32
  66.8 7.3 %collective-permute-start.32 = (bf16[256,256]{1,0:T(8,128)(2,1)S(1)}, bf16[256,256]{1,0:T(8,128)(2,1)S(1)}, u32[]{:S(2)}, u32[]{:S(2)}) collective-permute-start(bf16[256,256]{1,0:T(8,128)(2,1)S(1)} %get-tuple-element.46.refs_0_), channel_id=1, source_target_pairs={{0,16},{8,24},{16,0},{24,8},{1,17},{9,25},{17,1},{25,9},{2,18},{10... | collective-permute-start | bytes 393224 | tf_op jit(solution)/shard_map/ppermute | solution.py:32
  66.8 13.3 %collective-permute-start.33 = (bf16[256,256]{1,0:T(8,128)(2,1)S(1)}, bf16[256,256]{1,0:T(8,128)(2,1)S(1)}, u32[]{:S(2)}, u32[]{:S(2)}) collective-permute-start(bf16[256,256]{1,0:T(8,128)(2,1)S(1)} %get-tuple-element.46.refs_0_), channel_id=1, source_target_pairs={{0,8},{8,0},{16,24},{24,16},{1,9},{9,1},{17,25},{25,17},{2,10},{10... | collective-permute-start | bytes 393224 | tf_op jit(solution)/shard_map/ppermute | solution.py:32
  70.2 9.9 %collective-permute-start.34 = (bf16[256,256]{1,0:T(8,128)(2,1)S(1)}, bf16[256,256]{1,0:T(8,128)(2,1)S(1)}, u32[]{:S(2)}, u32[]{:S(2)}) collective-permute-start(bf16[256,256]{1,0:T(8,128)(2,1)S(1)} %get-tuple-element.46.refs_0_), channel_id=1, source_target_pairs={{0,24},{8,16},{16,8},{24,0},{1,25},{9,17},{17,9},{25,1},{2,26},{10... | collective-permute-start | bytes 393224 | tf_op jit(solution)/shard_map/ppermute | solution.py:32
  70.6 9.5 %collective-permute-start.35 = (bf16[256,256]{1,0:T(8,128)(2,1)S(1)}, bf16[256,256]{1,0:T(8,128)(2,1)S(1)}, u32[]{:S(2)}, u32[]{:S(2)}) collective-permute-start(bf16[256,256]{1,0:T(8,128)(2,1)S(1)} %collective-permute-done.31.refs_1_), channel_id=1, source_target_pairs={{0,16},{8,24},{16,0},{24,8},{1,17},{9,25},{17,1},{25,9},{2,18},{10... | collective-permute-start | bytes 393224 | tf_op jit(solution)/shard_map/ppermute | solution.py:32
  74.1 10.1 %collective-permute-start.37 = (bf16[256,256]{1,0:T(8,128)(2,1)S(1)}, bf16[256,256]{1,0:T(8,128)(2,1)S(1)}, u32[]{:S(2)}, u32[]{:S(2)}) collective-permute-start(bf16[256,256]{1,0:T(8,128)(2,1)S(1)} %collective-permute-done.31.refs_1_), channel_id=1, source_target_pairs={{0,24},{8,16},{16,8},{24,0},{1,25},{9,17},{17,9},{25,1},{2,26},{10... | collective-permute-start | bytes 393224 | tf_op jit(solution)/shard_map/ppermute | solution.py:32
  84.3 21.2 %collective-permute-start.38 = (bf16[10,256,256]{2,1,0:T(8,128)(2,1)S(1)}, bf16[10,256,256]{2,1,0:T(8,128)(2,1)S(1)}, u32[]{:S(2)}, u32[]{:S(2)}) collective-permute-start(bf16[10,256,256]{2,1,0:T(8,128)(2,1)S(1)} %bundle.7.refs_0_), channel_id=1, source_target_pairs={{0,1},{1,0},{2,3},{3,2},{4,5},{5,4},{6,7},{7,6},{8,9},{9,8},{10,11... | collective-permute-start | bytes 3932168 | tf_op jit(solution)/shard_map/ppermute | solution.py:32
  89.4 10.0 %collective-permute-start.22 = (bf16[256,256]{1,0:T(8,128)(2,1)S(1)}, bf16[256,256]{1,0:T(8,128)(2,1)S(1)}, u32[]{:S(2)}, u32[]{:S(2)}) collective-permute-start(bf16[256,256]{1,0:T(8,128)(2,1)S(1)} %collective-permute-done.21.refs_3_), channel_id=1, source_target_pairs={{0,16},{8,24},{16,0},{24,8},{1,17},{9,25},{17,1},{25,9},{2,18},{10... | collective-permute-start | bytes 393224 | tf_op jit(solution)/shard_map/ppermute | solution.py:32
  92.6 8.7 %collective-permute-start.23 = (bf16[256,256]{1,0:T(8,128)(2,1)S(1)}, bf16[256,256]{1,0:T(8,128)(2,1)S(1)}, u32[]{:S(2)}, u32[]{:S(2)}) collective-permute-start(bf16[256,256]{1,0:T(8,128)(2,1)S(1)} %collective-permute-done.21.refs_3_), channel_id=1, source_target_pairs={{0,8},{8,0},{16,24},{24,16},{1,9},{9,1},{17,25},{25,17},{2,10},{10... | collective-permute-start | bytes 393224 | tf_op jit(solution)/shard_map/ppermute | solution.py:32
  95.9 11.3 %collective-permute-start.30 = (bf16[3,256,256]{2,1,0:T(8,128)(2,1)S(1)}, bf16[3,256,256]{2,1,0:T(8,128)(2,1)S(1)}, u32[]{:S(2)}, u32[]{:S(2)}) collective-permute-start(bf16[3,256,256]{2,1,0:T(8,128)(2,1)S(1)} %bundle.6.refs_0_), channel_id=1, source_target_pairs={{0,1},{1,0},{2,3},{3,2},{4,5},{5,4},{6,7},{7,6},{8,9},{9,8},{10,11... | collective-permute-start | bytes 1179656 | tf_op jit(solution)/shard_map/ppermute | solution.py:32
  (19 other events, 156.1 us)
